TPU v7x, 256 devices: a whole 4x4x8 slice. The times are simulated.
256 devices in a mesh: tm: 8 (over x_hi, y), rows: 32 (over x_lo, z, core).
Axes of the slice: x: 4 (x_hi: 2, x_lo: 2; x = x_hi * 2 + x_lo), y: 4, z: 8, core: 2. Of those that a mesh axis runs over, the one named last changes fastest.
Arguments:
- record: bfloat16 [2, 65536, 4096], P(None, 'rows', 'tm'), may hold values from -6 to 6
- seed_list: int32 [4], replicated, may hold values from 0 to 65535
- block_offsets: int32 [2], replicated, may hold values from 0 to 1048575
Outputs:
- range_sketch: float32 [65536, 128], P('rows')
- corange_sketch: float32 [2, 256, 4096], P(None, 'rows', 'tm')
- core_sketch: float32 [384, 384], P('rows')
Inputs may be any that keep to these rules, and one draw needn't show every extreme that they name: `seed_list`: entries 0, 1, 2, 3 seed the range, co-range, core row and core column test matrices.
All inputs are finite; a program needn't handle non-finite values.
Results may differ from a plain program's by a relative error of at most 0.0041.
Values sent between devices are 32-bit elements; how exact they have to be, the bound alone decides.
A program may use at most 64 MiB of HBM per device.

v0:
```python
import math

import jax
import jax.numpy as jnp
from jax import lax
from jax.sharding import PartitionSpec as P

RANGE = 128
CORANGE = 256
CORE = 384


def in_blocks(x, dim, size):
    before, after = (x.shape[:dim], x.shape[dim + 1 :])
    return jnp.moveaxis(x.reshape(*before, size, -1, *after), dim, 0)


def sum_at_owner(x, axis, dim):
    parts = in_blocks(x, dim, lax.axis_size(axis))
    arrived = lax.all_to_all(parts, axis, split_axis=0, concat_axis=0, tiled=True)
    return arrived.sum(axis=0)


def from_everyone(x, axis):
    size = lax.axis_size(axis)
    return lax.all_to_all(jnp.broadcast_to(x[None], (size, *x.shape)), axis, 0, 0, tiled=True)


def taken_together(x, axis):
    return from_everyone(x, axis).sum(axis=0)


def shift_down(values, amount):
    return lax.shift_right_logical(values, jnp.full(values.shape, amount, jnp.int32))


def sketch_matrix(seed_value, first_ids, second_ids, factor):
    hashed = (
        first_ids[:, None] * 668265263 + second_ids[None, :] * 374761393 + seed_value * 625341585
    )
    hashed = jnp.bitwise_xor(hashed, shift_down(hashed, 15))
    hashed = hashed * 739982445
    hashed = jnp.bitwise_xor(hashed, shift_down(hashed, 12))
    hashed = hashed * 695872825
    hashed = jnp.bitwise_xor(hashed, shift_down(hashed, 15))
    byte_sum = jnp.bitwise_and(hashed, 255)
    byte_sum = byte_sum + jnp.bitwise_and(shift_down(hashed, 8), 255)
    byte_sum = byte_sum + jnp.bitwise_and(shift_down(hashed, 16), 255)
    byte_sum = byte_sum + jnp.bitwise_and(shift_down(hashed, 24), 255)
    return ((byte_sum - 510).astype(jnp.float32) * factor).astype(jnp.bfloat16)


def sum_range(part):
    return lax.psum(part, "tm")


def sum_corange(parts):
    return sum_at_owner(parts, "rows", 1)


def sum_core(part):
    share = sum_at_owner(part, "rows", 0)
    return taken_together(share, "tm")


def shards(record, seed_list, block_offsets):
    blocks, rows_dev, cols_dev = record.shape
    rows_count = lax.axis_size("rows")
    time_count = lax.axis_size("tm")
    row_factor = 1.0 / (147.8 * math.sqrt(rows_dev * rows_count))
    col_factor = 1.0 / (147.8 * math.sqrt(blocks * cols_dev * time_count))
    row_ids = lax.axis_index("rows") * rows_dev + jnp.arange(rows_dev, dtype=jnp.int32)
    psi_rows = sketch_matrix(
        seed_list[1], jnp.arange(CORANGE, dtype=jnp.int32), row_ids, row_factor
    )
    phi_rows = sketch_matrix(seed_list[2], jnp.arange(CORE, dtype=jnp.int32), row_ids, row_factor)
    col_base = lax.axis_index("tm") * cols_dev + jnp.arange(cols_dev, dtype=jnp.int32)
    range_local = jnp.zeros((rows_dev, RANGE), jnp.float32)
    core_local = jnp.zeros((CORE, CORE), jnp.float32)
    range_sketch = None
    core_sketch = None
    corange_parts = []
    for number in range(blocks):
        matrix = record[number]
        col_ids = block_offsets[number] + col_base
        omega_cols = sketch_matrix(
            seed_list[0], col_ids, jnp.arange(RANGE, dtype=jnp.int32), col_factor
        )
        xi_cols = sketch_matrix(
            seed_list[3], jnp.arange(CORE, dtype=jnp.int32), col_ids, col_factor
        )
        range_part = jnp.dot(matrix, omega_cols, preferred_element_type=jnp.float32)
        corange_part = jnp.dot(psi_rows, matrix, preferred_element_type=jnp.float32)
        projected = jnp.dot(phi_rows, matrix, preferred_element_type=jnp.float32)
        core_part = jnp.dot(
            projected, xi_cols.astype(jnp.float32).T, precision=lax.Precision.HIGHEST
        )
        range_local = range_local + range_part
        core_local = core_local + core_part
        corange_parts.append(corange_part)
    range_sketch = sum_range(range_local)
    core_sketch = sum_core(core_local)
    corange_sketch = sum_corange(jnp.stack(corange_parts))
    return (range_sketch, corange_sketch, core_sketch)


def solution(mesh):
    placed = (P(None, "rows", "tm"), P(), P())
    return jax.shard_map(
        shards,
        mesh=mesh,
        in_specs=placed,
        out_specs=(P("rows", None), P(None, "rows", "tm"), P("rows", None)),
        check_vma=False,
    )
```

profile of v0, /device:TPU:32, one launch (start us, length us, event | category | flops | bytes accessed | tf_op | source)
XLA Modules:
  0.0 185.7 jit_solution(12413052100564470267)
XLA Ops:
  7.2 1.5 fusion.175
  9.3 0.0 copy-start.1
  9.3 4.2 %fusion.9 = f32[384,512]{1,0:T(8,128)S(1)} fusion(bf16[2,2048,512]{2,1,0:T(8,128)(2,1)} %param.3, s32[]{:T(128)} %bitcast.12, s32[2048]{0:T(1024)S(1)} %add_multiply_fusion.1, s32[384]{0:T(512)S(1)} %iota_multiply_fusion), kind=kOutput, calls=%fused_computation.17 | convolution fusion | flops 824180736 | bytes 2893824 | tf_op jit(solution)/shard_map/dot_general | solution.py:94
  13.5 0.0 copy-done.1
  13.5 0.0 copy-start
  13.5 2.5 %fusion.12 = f32[384,512]{1,0:T(8,128)S(1)} fusion(bf16[2,2048,512]{2,1,0:T(8,128)(2,1)S(1)} %copy-done.1, s32[]{:T(128)} %bitcast.12, s32[2048]{0:T(1024)S(1)} %add_multiply_fusion.1, s32[384]{0:T(512)S(1)} %iota_multiply_fusion), kind=kOutput, calls=%fused_computation.20 | convolution fusion | flops 824180736 | bytes 2893828 | tf_op jit(solution)/shard_map/dot_general | solution.py:94
  16.0 0.0 copy-done
  16.0 0.6 fusion.176
  17.3 1.3 fusion.91
  18.6 1.4 fusion.32
  20.0 1.4 convolution_add_fusion.1
  21.3 0.9 reshape.121
  22.3 9.7 %all-to-all-start.1 = ((f32[32,12,384]{2,1,0:T(8,128)}), f32[32,12,384]{2,1,0:T(8,128)S(1)}, u32[]{:S(2)}, u32[]{:S(2)}) async-start(f32[32,12,384]{2,1,0:T(8,128)} %reshape.121), calls=%async_computation.1 | async-start | bytes 1572864 | tf_op jit(solution)/shard_map/all_to_all | solution.py:20
  32.6 0.0 copy-start.2
  32.6 3.4 %fusion.25 = f32[1,32,8,512]{3,2,1,0:T(8,128)S(1)} fusion(bf16[2,2048,512]{2,1,0:T(8,128)(2,1)} %param.3, s32[]{:T(128)} %bitcast.6, s32[2048]{0:T(1024)S(1)} %add_multiply_fusion.1, s32[32,8]{1,0:T(8,128)S(1)} %add_multiply_fusion), kind=kOutput, calls=%fused_computation.33 | convolution fusion | flops 549453824 | bytes 2631168 | tf_op jit(solution)/shard_map/dot_general | solution.py:93
  36.0 0.0 copy-done.2
  36.0 1.7 fusion.22
  37.7 17.6 %all-to-all-done.1 = f32[32,12,384]{2,1,0:T(8,128)S(1)} async-done(((f32[32,12,384]{2,1,0:T(8,128)}), f32[32,12,384]{2,1,0:T(8,128)S(1)}, u32[]{:S(2)}, u32[]{:S(2)}) %all-to-all-start.1) | async-done | bytes 589856 | tf_op jit(solution)/shard_map/all_to_all | solution.py:20
  55.3 0.1 reduce_sum.28
  55.4 0.7 broadcast_in_dim.50
  56.0 6.6 %all-to-all-start.2 = ((f32[8,12,384]{2,1,0:T(8,128)}), f32[8,12,384]{2,1,0:T(8,128)S(1)}, u32[]{:S(2)}, u32[]{:S(2)}) async-start(f32[8,12,384]{2,1,0:T(8,128)} %broadcast_in_dim.50), calls=%async_computation.2 | async-start | bytes 393216 | tf_op jit(solution)/shard_map/all_to_all | solution.py:26
  62.7 0.1 maximum_bitcast_fusion
  62.8 1.1 copy.12
  63.8 7.3 %all-to-all-done.2 = f32[8,12,384]{2,1,0:T(8,128)S(1)} async-done(((f32[8,12,384]{2,1,0:T(8,128)}), f32[8,12,384]{2,1,0:T(8,128)S(1)}, u32[]{:S(2)}, u32[]{:S(2)}) %all-to-all-start.2) | async-done | bytes 147488 | tf_op jit(solution)/shard_map/all_to_all | solution.py:26
  71.1 3.8 %all-to-all-start = ((f32[32,2,8,512]{3,2,1,0:T(8,128)}), f32[32,2,8,512]{3,2,1,0:T(8,128)S(1)}, u32[]{:S(2)}, u32[]{:S(2)}) async-start(f32[32,2,8,512]{3,2,1,0:T(8,128)} %copy.12), calls=%async_computation | async-start | bytes 2097152 | tf_op jit(solution)/shard_map/all_to_all | solution.py:20
  74.9 0.0 all-reduce.2.cloned.1.call-start
  75.6 1.3 fusion.92
  76.9 2.6 %fusion.14 = f32[128,2048]{1,0:T(8,128)S(1)} fusion(bf16[2,2048,512]{2,1,0:T(8,128)(2,1)} %param.3, s32[]{:T(128)} %bitcast.1, s32[128]{0:T(128)S(1)} %iota_multiply_fusion.1, s32[512]{0:T(512)S(1)} %get-tuple-element.26), kind=kOutput, calls=%fused_computation.22 | convolution fusion | flops 270008320 | bytes 3148800 | tf_op jit(solution)/shard_map/dot_general | solution.py:92
  79.5 3.6 %fusion.2 = f32[2048,128]{0,1:T(8,128)} fusion(f32[128,2048]{1,0:T(8,128)S(1)} %fusion.14, bf16[2,2048,512]{2,1,0:T(8,128)(2,1)} %param.3, s32[512]{0:T(512)S(1)} %get-tuple-element.27, s32[]{:T(128)} %bitcast.1, s32[128]{0:T(128)S(1)} %iota_multiply_fusion.1), kind=kOutput, calls=%fused_computation.10 | convolution fusion | flops 270270464 | bytes 4197376 | tf_op jit(solution)/shard_map/dot_general | solution.py:92
  83.1 0.0 all-reduce.2.cloned.1.call-update
  83.2 91.9 %all-reduce.2.cloned.1.call-done = f32[2048,128]{0,1:T(8,128)} async-done(((f32[2048,128]{0,1:T(8,128)}), f32[2048,128]{0,1:T(8,128)}) %all-reduce.2.cloned.1.call-update) | async-done | bytes 1048592 | tf_op jit(solution)/shard_map/psum | solution.py:54
  175.0 2.5 %copy.14 = f32[2048,128]{1,0:T(8,128)} copy(f32[2048,128]{0,1:T(8,128)} %all-reduce.2.cloned.1.call-done) | data formatting | bytes 2097152
  177.6 0.6 reduce_sum.29
  178.2 0.0 all-to-all-done
  178.2 0.7 reduce_sum.27
  (4 shorter events, 0.0 us)
Async XLA Ops:
  9.3 4.2 %copy-start.1 = (bf16[2,2048,512]{2,1,0:T(8,128)(2,1)S(1)}, bf16[2,2048,512]{2,1,0:T(8,128)(2,1)}, u32[]{:S(2)}) copy-start(bf16[2,2048,512]{2,1,0:T(8,128)(2,1)} %param.3) | copy-start | bytes 12582916
  13.5 2.5 %copy-start = (s32[2]{0:T(128)S(1)}, s32[2]{0:T(128)}, u32[]{:S(2)}) copy-start(s32[2]{0:T(128)} %param.5) | copy-start | bytes 28
  22.3 33.0 %all-to-all-start.1 = ((f32[32,12,384]{2,1,0:T(8,128)}), f32[32,12,384]{2,1,0:T(8,128)S(1)}, u32[]{:S(2)}, u32[]{:S(2)}) async-start(f32[32,12,384]{2,1,0:T(8,128)} %reshape.121), calls=%async_computation.1 | async-start | bytes 1572864 | tf_op jit(solution)/shard_map/all_to_all | solution.py:20
  32.6 3.4 %copy-start.2 = (bf16[2,2048,512]{2,1,0:T(8,128)(2,1)S(1)}, bf16[2,2048,512]{2,1,0:T(8,128)(2,1)}, u32[]{:S(2)}) copy-start(bf16[2,2048,512]{2,1,0:T(8,128)(2,1)} %param.3) | copy-start | bytes 12582916
  56.0 15.1 %all-to-all-start.2 = ((f32[8,12,384]{2,1,0:T(8,128)}), f32[8,12,384]{2,1,0:T(8,128)S(1)}, u32[]{:S(2)}, u32[]{:S(2)}) async-start(f32[8,12,384]{2,1,0:T(8,128)} %broadcast_in_dim.50), calls=%async_computation.2 | async-start | bytes 393216 | tf_op jit(solution)/shard_map/all_to_all | solution.py:26
  71.1 107.1 %all-to-all-start = ((f32[32,2,8,512]{3,2,1,0:T(8,128)}), f32[32,2,8,512]{3,2,1,0:T(8,128)S(1)}, u32[]{:S(2)}, u32[]{:S(2)}) async-start(f32[32,2,8,512]{3,2,1,0:T(8,128)} %copy.12), calls=%async_computation | async-start | bytes 2097152 | tf_op jit(solution)/shard_map/all_to_all | solution.py:20
  74.9 100.1 %all-reduce.2.cloned.1.call-start = ((), (), s32[]{:S(2)}) async-start(), calls=%async_computation.3 | async-start | bytes 2097152 | tf_op jit(solution)/shard_map/psum | solution.py:54
Sparse Core Ops, SparseCore 0:
  83.3 91.7 all-reduce.1
where the time goes:
time: 186 us
  waiting for transfers between devices  117 us (63%)
  matrix products  20.8 us (11%)
  starting transfers between devices  20.1 us (11%)
  between operations  16.8 us (9%)
  local copies, waits for them, and re-layouts  7.35 us (4%)
  other arithmetic  3.97 us (2%)
    psum x1, waiting for transfers between devices, sum_range(): return lax.psum(part, 'tm')  91.9 us
    all_to_all x2, waiting for transfers between devices, sum_at_owner(): lax.all_to_all(parts, axis, split_axis=0, concat_axis=0, tiled=True)  17.6 us
    all_to_all x2, starting transfers between devices, sum_at_owner(): lax.all_to_all(parts, axis, split_axis=0, concat_axis=0, tiled=True)  13.4 us
    all_to_all x1, waiting for transfers between devices, from_everyone(): lax.all_to_all(jnp.broadcast_to(x[None], (size, *x.shape)), axis, 0, 0, t...  7.3 us
    dot_general x2, matrix products, shards(): projected = jnp.dot(phi_rows, matrix, preferred_element_type=jnp.float32)  6.71 us
    all_to_all x1, starting transfers between devices, from_everyone(): lax.all_to_all(jnp.broadcast_to(x[None], (size, *x.shape)), axis, 0, 0, t...  6.64 us
    dot_general x2, matrix products, shards(): range_part = jnp.dot(matrix, omega_cols, preferred_element_type=jnp.float32)  6.24 us
    dot_general x2, matrix products, shards(): corange_part = jnp.dot(psi_rows, matrix, preferred_element_type=jnp.float32)  5.1 us
  transfers between devices with their start and end apart: 4, of which 3 were waited for; matrix products, arithmetic and copies ran while one was open for 9% of the time, Pallas kernels for 0%

commit v1 on v0

v1 whole, which is shorter than its diff:
```python
import functools
import math

import jax
import jax.numpy as jnp
from jax import lax
from jax.experimental import pallas as pl
from jax.experimental.pallas import tpu as pltpu
from jax.sharding import PartitionSpec as P

RANGE = 128
CORANGE = 256
CORE = 384
C_A = 668265263
C_B = 374761393
C_S = 625341585
MESH = pl.DeviceIdType.MESH

YS = 4
ZS = 8
STREAMS = 2
HALF_PSI = CORANGE // 2
HALF_PHI = CORE // 2
HALF = HALF_PSI + HALF_PHI
KC = 512


def srl(values, amount):
    return lax.shift_right_logical(values, jnp.full(values.shape, amount, jnp.int32))


def gauss(base, factor):
    h = base ^ srl(base, 15)
    h = h * 739982445
    h = h ^ srl(h, 12)
    h = h * 695872825
    h = h ^ srl(h, 15)
    pairs = (h & 0x00FF00FF) + (srl(h, 8) & 0x00FF00FF)
    total = (pairs + srl(pairs, 16)) & 0x7FF
    return ((total - 510).astype(jnp.float32) * factor).astype(jnp.bfloat16)


def wrapped(number):
    return (number + (1 << 31)) % (1 << 32) - (1 << 31)


def iota(shape, dim):
    return lax.broadcasted_iota(jnp.int32, shape, dim)


def kernel(
    row_factor, col_factor, rows_dev, cols_dev,
    seeds, offsets, record,
    range_out, corange_out, core_out,
    rec, omega, xit, ids, lhs0, lhs1, acc_a, acc_b, core_a, core_b,
    part, rb1, rb2, rb3, fwd, ysum, xb,
    got_cor, got_core, zr_cor, zr_core, zs_cor, zs_core, xl_cor, xl_core, tmb,
    in_sem, s1s, s1r, s2s, s2r, s3s, s3r, xs, xr, g1s, g1r, g2s, g2r,
    ds, dr, zs, zr, ls, lr, ts, tr,
):
    tm, rw = lax.axis_index("tm"), lax.axis_index("rows")
    xh, y = tm // YS, lax.rem(tm, YS)
    xl, z, c = rw // (2 * ZS), lax.rem(rw // 2, ZS), lax.rem(rw, 2)

    def device(xh=xh, y=y, xl=xl, z=z, c=c):
        return (xh * YS + y, xl * (2 * ZS) + z * 2 + c)

    y_right, y_left = lax.rem(y + 1, YS), lax.rem(y + YS - 1, YS)
    y_far = lax.rem(y + 2, YS)
    right, left = device(y=y_right), device(y=y_left)
    x_peer = device(xh=1 - xh)
    xl_peer = device(xl=1 - xl)
    partner = device(c=1 - c)
    z_up, z_down = device(z=lax.rem(z + 1, ZS)), device(z=lax.rem(z + ZS - 1, ZS))
    tm_peers = [(lax.rem(tm + i, 2 * YS), rw) for i in range(1, 2 * YS)]

    barrier = pltpu.get_barrier_semaphore()
    greeted = [partner, z_up, z_down, xl_peer, *tm_peers]
    for other in greeted:
        pl.semaphore_signal(barrier, inc=1, device_id=other, device_id_type=MESH)

    chunk = rows_dev // YS
    run = chunk // STREAMS // 2

    def rows_of(d, s, half=None):
        if half is None:
            return pl.ds(pl.multiple_of(d * chunk + s * 2 * run, run), 2 * run)
        return pl.ds(pl.multiple_of(d * chunk + (s * 2 + half) * run, run), run)

    order = [y_far, y_right, y_left, y]
    loads = []
    for i, d in enumerate(order):
        where = pl.ds(pl.multiple_of(d * chunk, chunk), chunk)
        load = pltpu.make_async_copy(record.at[:, where, :], rec.at[:, where, :], in_sem.at[i])
        load.start()
        loads.append(load)

    def send(src, dst, ssem, rsem, to):
        copy = pltpu.make_async_remote_copy(
            src, dst, ssem, rsem, device_id=to, device_id_type=MESH
        )
        copy.start()
        return copy

    sent = []

    lanes = iota((64, 128), 1)
    subs = iota((64, 128), 0)
    pattern_o = subs * C_A + lanes * C_B
    pattern_x = subs * C_B + lanes * C_A
    blocks = 2
    for k in range(blocks):
        col0 = offsets[k] + tm * cols_dev

        def omega_rows(i, _, k=k, col0=col0):
            base = pattern_o + ((col0 + i * 64) * C_A + seeds[0] * C_S)
            omega[pl.ds(pl.multiple_of(k * cols_dev + i * 64, 64), 64), :] = gauss(base, col_factor)
            return 0

        lax.fori_loop(0, cols_dev // 64, omega_rows, 0)

    def range_chunk(d):
        def block(i, _):
            where = pl.ds(pl.multiple_of(d * chunk + i * 256, 256), 256)
            part[where, :] = jnp.dot(
                rec[0, where, :], omega[0:cols_dev, :], preferred_element_type=jnp.float32
            ) + jnp.dot(
                rec[1, where, :], omega[cols_dev : 2 * cols_dev, :], preferred_element_type=jnp.float32
            )
            return 0

        lax.fori_loop(0, chunk // 256, block, 0)

    loads[0].wait()
    range_chunk(y_far)
    pl.semaphore_wait(barrier, len(greeted))
    S1, S2, S3, XC, G1, G2 = {}, {}, {}, {}, {}, {}
    for s in range(STREAMS):
        S1[s, 0] = send(part.at[rows_of(y_far, s, 0)], rb1.at[s, 0], s1s.at[s, 0], s1r.at[s, 0], right)
        S1[s, 1] = send(part.at[rows_of(y_far, s, 1)], rb1.at[s, 1], s1s.at[s, 1], s1r.at[s, 1], left)
    loads[1].wait()
    range_chunk(y_right)
    loads[2].wait()
    range_chunk(y_left)
    for s in range(STREAMS):
        S2[s, 0] = send(part.at[rows_of(y_right, s, 1)], rb2.at[s, 0], s2s.at[s, 0], s2r.at[s, 0], right)
        S2[s, 1] = send(part.at[rows_of(y_left, s, 0)], rb2.at[s, 1], s2s.at[s, 1], s2r.at[s, 1], left)
    loads[3].wait()
    range_chunk(y)

    def range_forward(s):
        S1[s, 0].wait_recv()
        fwd[s, 0] = part[rows_of(y_right, s, 0), :] + rb1[s, 0]
        S3[s, 0] = send(fwd.at[s, 0], rb3.at[s, 0], s3s.at[s, 0], s3r.at[s, 0], right)
        S1[s, 1].wait_recv()
        fwd[s, 1] = part[rows_of(y_left, s, 1), :] + rb1[s, 1]
        S3[s, 1] = send(fwd.at[s, 1], rb3.at[s, 1], s3s.at[s, 1], s3r.at[s, 1], left)

    def range_cross(s):
        S2[s, 0].wait_recv()
        S2[s, 1].wait_recv()
        S3[s, 0].wait_recv()
        S3[s, 1].wait_recv()
        ysum[s, 0:run] = part[rows_of(y, s, 0), :] + rb3[s, 0] + rb2[s, 1]
        ysum[s, run : 2 * run] = part[rows_of(y, s, 1), :] + rb2[s, 0] + rb3[s, 1]
        XC[s] = send(ysum.at[s], xb.at[s], xs.at[s], xr.at[s], x_peer)

    def range_spread(s):
        XC[s].wait_recv()
        own = rows_of(y, s)
        range_out[own, :] = ysum[s] + xb[s]
        G1[s, 0] = send(range_out.at[own], range_out.at[own], g1s.at[s, 0], g1r.at[s, 0], right)
        G1[s, 1] = send(range_out.at[own], range_out.at[own], g1s.at[s, 1], g1r.at[s, 1], left)

    def range_relay(s):
        G1[s, 0].wait_recv()
        a = rows_of(y_left, s, 0)
        G2[s, 0] = send(range_out.at[a], range_out.at[a], g2s.at[s, 0], g2r.at[s, 0], right)
        G1[s, 1].wait_recv()
        b = rows_of(y_right, s, 1)
        G2[s, 1] = send(range_out.at[b], range_out.at[b], g2s.at[s, 1], g2r.at[s, 1], left)

    def range_end(s):
        G2[s, 0].wait_recv()
        G2[s, 1].wait_recv()

    for k in range(blocks):
        col0 = offsets[k] + tm * cols_dev

        def xi_rows(i, _, k=k, col0=col0):
            at = pl.ds(pl.multiple_of(k * cols_dev + i * 64, 64), 64)
            for g in range(CORE // 128):
                base = pattern_x + ((col0 + i * 64) * C_B + seeds[3] * C_S + wrapped(g * 128 * C_A))
                xit[at, g * 128 : (g + 1) * 128] = gauss(base, col_factor)
            return 0

        lax.fori_loop(0, cols_dev // 64, xi_rows, 0)

    row0 = rw * rows_dev

    def row_ids(owner_core):
        m = iota((HALF_PSI, 128), 0)
        at_z, rest = m >> 4, m & 15
        psi_id = (rest >> 3) * 128 + at_z * 16 + owner_core * 8 + (rest & 7)
        ids[0:HALF_PSI, :] = psi_id * C_A + iota((HALF_PSI, 128), 1) * C_B + seeds[1] * C_S
        m = iota((HALF_PHI, 128), 0)
        at_z = (m * 2731) >> 16
        rest = m - at_z * 24
        at_x = jnp.where(rest >= 12, 1, 0)
        phi_id = (at_x * (2 * ZS) + at_z * 2 + owner_core) * 12 + (rest - at_x * 12)
        ids[HALF_PSI:HALF, :] = phi_id * C_A + iota((HALF_PHI, 128), 1) * C_B + seeds[2] * C_S

    def hash_chunk(kc, lhs):
        for g in range(KC // 128):
            shift = (row0 + (kc * KC + g * 128)) * C_B
            for r in range(0, HALF, 64):
                lhs[r : r + 64, g * 128 : (g + 1) * 128] = gauss(ids[r : r + 64, :] + shift, row_factor)

    def dot_chunk(kc, lhs, acc):
        for k in range(blocks):
            for n in range(0, cols_dev, 256):
                got = jnp.dot(
                    lhs[...], rec[k, kc * KC : (kc + 1) * KC, n : n + 256], preferred_element_type=jnp.float32
                )
                at = slice(k * cols_dev + n, k * cols_dev + n + 256)
                if kc == 0:
                    acc[:, at] = got
                else:
                    acc[:, at] += got

    def core_dot(acc, core):
        for r in range(0, HALF_PHI, 64):
            rows = acc[HALF_PSI + r : HALF_PSI + r + 64, :]
            high = rows.astype(jnp.bfloat16)
            low = (rows - high.astype(jnp.float32)).astype(jnp.bfloat16)
            core[r : r + 64, :] = jnp.dot(high, xit[...], preferred_element_type=jnp.float32) + jnp.dot(
                low, xit[...], preferred_element_type=jnp.float32
            )

    n_chunks = rows_dev // KC

    def half(owner_core, acc, core, events):
        row_ids(owner_core)
        hash_chunk(0, lhs0)
        for kc in range(n_chunks):
            if kc + 1 < n_chunks:
                hash_chunk(kc + 1, (lhs0, lhs1)[(kc + 1) % 2])
            dot_chunk(kc, (lhs0, lhs1)[kc % 2], acc)
            for event in events.get(kc, ()):
                event()
        core_dot(acc, core)

    half(1 - c, acc_a, core_a, {})
    D = [
        send(acc_a.at[0:HALF_PSI], got_cor, ds.at[0], dr.at[0], partner),
        send(core_a, got_core, ds.at[1], dr.at[1], partner),
    ]
    for s in range(STREAMS):
        range_forward(s)
    half(c, acc_b, core_b, {1: [functools.partial(range_cross, s) for s in range(STREAMS)]})
    for copy in D:
        copy.wait_recv()

    Z = {}

    def z_step(step, up):
        d = lax.rem(z + (5 - step) if up else z + ZS - 5 + step, ZS)
        way = 0 if up else 1
        cor_at = pl.ds(pl.multiple_of(d * 16, 16), 16)
        core_at = pl.ds(pl.multiple_of(d * 24, 8), 24)
        cor = acc_b[cor_at, :] + got_cor[cor_at, :]
        core = core_b[core_at, :] + got_core[core_at, :]
        to = z_up if up else z_down
        i = step - 1
        half_cols = slice(0, cols_dev) if up else slice(cols_dev, 2 * cols_dev)
        half_rows = slice(0, 16) if up else slice(16, 24)
        if step > 1:
            for copy in Z[step - 1, way]:
                copy.wait_recv()
        zs_cor[way, i] = cor
        zs_core[way, i] = core
        if step == 2:
            zs_cor[way, i, :, half_cols] += zr_cor[way, 0, :, half_cols]
            zs_core[way, i, half_rows, :] += zr_core[way, 0, half_rows, :]
        elif step > 2:
            zs_cor[way, i] += zr_cor[way, i - 1]
            zs_core[way, i] += zr_core[way, i - 1]
        cor_pick = (way, i, slice(None), half_cols) if step == 1 else (way, i)
        core_pick = (way, i, half_rows) if step == 1 else (way, i)
        Z[step, way] = [
            send(zs_cor.at[cor_pick], zr_cor.at[cor_pick], zs.at[way, i, 0], zr.at[way, i, 0], to),
            send(zs_core.at[core_pick], zr_core.at[core_pick], zs.at[way, i, 1], zr.at[way, i, 1], to),
        ]

    z_step(1, True)
    z_step(1, False)
    for s in range(STREAMS):
        range_spread(s)
    z_step(2, True)
    z_step(2, False)
    z_step(3, True)
    z_step(3, False)
    for s in range(STREAMS):
        range_relay(s)
    z_step(4, True)
    z_step(4, False)
    own_cor = pl.ds(pl.multiple_of(z * 16, 16), 16)
    own_core = pl.ds(pl.multiple_of(z * 24, 8), 24)
    acc_b[own_cor, :] += got_cor[own_cor, :]
    core_b[own_core, :] += got_core[own_core, :]
    for way in range(2):
        for copy in Z[4, way]:
            copy.wait_recv()
    core_b[own_core, :] += zr_core[0, 3] + zr_core[1, 3]
    acc_b[own_cor, :] += zr_cor[0, 3] + zr_cor[1, 3]
    L = [
        send(core_b.at[own_core], xl_core, ls.at[1], lr.at[1], xl_peer),
        send(
            acc_b.at[pl.ds(pl.multiple_of(z * 16 + (1 - xl) * 8, 8), 8)], xl_cor, ls.at[0], lr.at[0], xl_peer
        ),
    ]
    L[0].wait_recv()
    both = core_b[own_core, :] + xl_core[...]
    share = jnp.where(xl == 0, both[0:12, :], both[12:24, :])
    tmb[tm, 0:12, :] = share
    tmb[tm, 12:16, :] = jnp.zeros((4, CORE), jnp.float32)
    T = [
        send(tmb.at[tm], tmb.at[tm], ts.at[i], tr.at[i], to) for i, to in enumerate(tm_peers)
    ]
    L[1].wait_recv()
    mine = acc_b[pl.ds(pl.multiple_of(z * 16 + xl * 8, 8), 8), :] + xl_cor[...]
    for k in range(blocks):
        corange_out[k] = mine[:, k * cols_dev : (k + 1) * cols_dev]
    for copy in T:
        copy.wait_recv()
    total = tmb[0, 0:12, :]
    for i in range(1, 2 * YS):
        total = total + tmb[i, 0:12, :]
    core_out[...] = total
    for s in range(STREAMS):
        range_end(s)
    for group in (S1, S2, S3, XC, G1, G2):
        for copy in group.values():
            copy.wait_send()
    for copy in [*D, *L, *T, *[copy for pair in Z.values() for copy in pair]]:
        copy.wait_send()


def shards(record, seed_list, block_offsets):
    blocks, rows_dev, cols_dev = record.shape
    rows_count, time_count = lax.axis_size("rows"), lax.axis_size("tm")
    row_factor = 1.0 / (147.8 * math.sqrt(rows_dev * rows_count))
    col_factor = 1.0 / (147.8 * math.sqrt(blocks * cols_dev * time_count))
    run = rows_dev // YS // STREAMS // 2
    f32, bf16 = jnp.float32, jnp.bfloat16
    vmem, dma = pltpu.VMEM, pltpu.SemaphoreType.DMA
    return pl.pallas_call(
        functools.partial(kernel, row_factor, col_factor, rows_dev, cols_dev),
        out_shape=(
            jax.ShapeDtypeStruct((rows_dev, RANGE), f32),
            jax.ShapeDtypeStruct((blocks, CORANGE // rows_count, cols_dev), f32),
            jax.ShapeDtypeStruct((CORE // rows_count, CORE), f32),
        ),
        in_specs=[
            pl.BlockSpec(memory_space=pltpu.SMEM),
            pl.BlockSpec(memory_space=pltpu.SMEM),
            pl.BlockSpec(memory_space=pl.ANY),
        ],
        out_specs=(pl.BlockSpec(memory_space=pltpu.VMEM),) * 3,
        scratch_shapes=[
            vmem((blocks, rows_dev, cols_dev), bf16),
            vmem((blocks * cols_dev, RANGE), bf16),
            vmem((blocks * cols_dev, CORE), bf16),
            vmem((HALF, 128), jnp.int32),
            vmem((HALF, KC), bf16),
            vmem((HALF, KC), bf16),
            vmem((HALF, blocks * cols_dev), f32),
            vmem((HALF, blocks * cols_dev), f32),
            vmem((HALF_PHI, CORE), f32),
            vmem((HALF_PHI, CORE), f32),
            vmem((rows_dev, RANGE), f32),
            vmem((STREAMS, 2, run, RANGE), f32),
            vmem((STREAMS, 2, run, RANGE), f32),
            vmem((STREAMS, 2, run, RANGE), f32),
            vmem((STREAMS, 2, run, RANGE), f32),
            vmem((STREAMS, 2 * run, RANGE), f32),
            vmem((STREAMS, 2 * run, RANGE), f32),
            vmem((HALF_PSI, blocks * cols_dev), f32),
            vmem((HALF_PHI, CORE), f32),
            vmem((2, 4, 16, blocks * cols_dev), f32),
            vmem((2, 4, 24, CORE), f32),
            vmem((2, 4, 16, blocks * cols_dev), f32),
            vmem((2, 4, 24, CORE), f32),
            vmem((8, blocks * cols_dev), f32),
            vmem((24, CORE), f32),
            vmem((2 * YS, 16, CORE), f32),
            dma((YS,)),
            *[dma((STREAMS, 2))] * 6,
            *[dma((STREAMS,))] * 2,
            *[dma((STREAMS, 2))] * 4,
            *[dma((2,))] * 2,
            *[dma((2, 4, 2))] * 2,
            *[dma((2,))] * 2,
            *[dma((2 * YS - 1,))] * 2,
        ],
        compiler_params=pltpu.CompilerParams(collective_id=0, has_side_effects=True),
        name="three_sketch",
    )(seed_list, block_offsets, record)


def solution(mesh):
    placed = (P(None, "rows", "tm"), P(), P())
    return jax.shard_map(
        shards,
        mesh=mesh,
        in_specs=placed,
        out_specs=(P("rows", None), P(None, "rows", "tm"), P("rows", None)),
        check_vma=False,
    )
```

time: 186 us -> 56.5 us (0.30)
  waiting for transfers between devices: 117 us -> 0 us
  Pallas kernels: 0 us -> 50.2 us
  matrix products: 20.8 us -> 0 us
  starting transfers between devices: 20.1 us -> 0 us
  between operations: 16.8 us -> 0.64 us
  other arithmetic: 3.97 us -> 0 us
  local copies, waits for them, and re-layouts: 7.35 us -> 4.98 us
    psum x1 -> x0, waiting for transfers between devices: 91.9 us -> none  [sum_range(): return lax.psum(part, 'tm')]
    pallas_call x0 -> x1, Pallas kernels: none -> 50.2 us  [shards(): pl.pallas_call(functools.partial(kernel, row_factor, col_factor, rows_dev...]
    all_to_all x3 -> x0, waiting for transfers between devices: 24.9 us -> none  [the longest x2 17.6 us: sum_at_owner(): lax.all_to_all(parts, axis, split_axis=0, concat_axis=0, tiled=True)]
    dot_general x8 -> x0, matrix products: 20.8 us -> none  [the longest x2 6.71 us: shards(): projected = jnp.dot(phi_rows, matrix, preferred_element_type=jnp.float32)]
    all_to_all x3 -> x0, starting transfers between devices: 20.1 us -> none  [the longest x2 13.4 us: sum_at_owner(): lax.all_to_all(parts, axis, split_axis=0, concat_axis=0, tiled=True)]
    mul x6 -> x0, other arithmetic: 2.54 us -> none  [the longest x3 1.27 us: sketch_matrix(): first_ids[:, None] * 668265263 + second_ids[None, :] * 374761393]
    unnamed x7 -> x3, local copies, waits for them, and re-layouts: 2.55 us -> 4.98 us
    slice x2 -> x0, local copies, waits for them, and re-layouts: 2.11 us -> none  [the longest x1 1.46 us: shards(): seed_list[3]]
  transfers between devices with their start and end apart: 4 -> 0, of which waited for: 3 -> 0; matrix products, arithmetic and copies ran while one was open for 9% -> 0% of each run, Pallas kernels for 0% -> 0%
where the time goes in v1:
time: 56.5 us; the launch traced here: 55.8 us
  Pallas kernels  50.2 us (89%)
  local copies, waits for them, and re-layouts  4.98 us (9%)
  between operations  0.64 us (1%)
    pallas_call x1, Pallas kernels, shards(): pl.pallas_call(functools.partial(kernel, row_factor, col_factor, rows_dev...  50.2 us
    unnamed x3, local copies, waits for them, and re-layouts  4.98 us

profile of v1, /device:TPU:32, one launch (start us, length us, event | category | flops | bytes accessed | tf_op | source)
XLA Modules:
  0.0 55.8 jit_solution(16764829474562791521)
XLA Ops:
  0.6 50.2 %three_sketch.1 = (f32[2048,128]{1,0:T(8,128)}, f32[2,8,512]{2,1,0:T(8,128)}, f32[12,384]{1,0:T(8,128)}) custom-call(s32[4]{0:T(128)} %seeds.1, s32[2]{0:T(128)} %offsets.1, bf16[2,2048,512]{2,1,0:T(8,128)(2,1)} %record.1), custom_call_target="tpu_custom_call" | custom-call | tf_op jit(solution)/shard_map/three_sketch/pallas_call | solution.py:357
  50.9 2.3 %copy.9 = f32[2048,128]{1,0:T(8,128)} copy(f32[2048,128]{1,0:T(8,128)} %get-tuple-element.6) | data formatting | bytes 2097152
  53.1 1.4 %copy.10 = f32[2,8,512]{2,1,0:T(8,128)} copy(f32[2,8,512]{2,1,0:T(8,128)} %get-tuple-element.7) | data formatting | bytes 65536
  54.5 1.3 %copy.11 = f32[12,384]{1,0:T(8,128)} copy(f32[12,384]{1,0:T(8,128)} %get-tuple-element.8) | data formatting | bytes 36864

commit v2 on v1

v2 whole, which is shorter than its diff:
```python
import functools
import math

import jax
import jax.numpy as jnp
from jax import lax
from jax.experimental import pallas as pl
from jax.experimental.pallas import tpu as pltpu
from jax.sharding import PartitionSpec as P

RANGE = 128
CORANGE = 256
CORE = 384
C_A = 668265263
C_B = 374761393
C_S = 625341585
MESH = pl.DeviceIdType.MESH

YS = 4
ZS = 8
STREAMS = 2
HALF_PSI = CORANGE // 2
HALF_PHI = CORE // 2
KC = 512


def srl(values, amount):
    return lax.shift_right_logical(values, jnp.full(values.shape, amount, jnp.int32))


def gauss(base, factor):
    h = base ^ srl(base, 15)
    h = h * 739982445
    h = h ^ srl(h, 12)
    h = h * 695872825
    h = h ^ srl(h, 15)
    pairs = (h & 0x00FF00FF) + (srl(h, 8) & 0x00FF00FF)
    total = (pairs + srl(pairs, 16)) & 0x7FF
    return ((total - 510).astype(jnp.float32) * factor).astype(jnp.bfloat16)


def wrapped(number):
    return (number + (1 << 31)) % (1 << 32) - (1 << 31)


def iota(shape, dim):
    return lax.broadcasted_iota(jnp.int32, shape, dim)


def kernel(
    row_factor, col_factor, rows_dev, cols_dev,
    seeds, offsets, record,
    range_out, corange_out, core_out,
    rec, omega, xit, ids, lhs0, lhs1, proj, cor, core,
    part, rb1, rb2, rb3, fwd, ysum, xb,
    got_cor, got_core, zr_cor, zr_core, zs_cor, zs_core, xl_cor, xl_core, tmb,
    in_sem, s1s, s1r, s2s, s2r, s3s, s3r, xs, xr, g1s, g1r, g2s, g2r,
    ds, dr, zs, zr, ls, lr, ts, tr,
):
    tm, rw = lax.axis_index("tm"), lax.axis_index("rows")
    xh, y = tm // YS, lax.rem(tm, YS)
    xl, z, c = rw // (2 * ZS), lax.rem(rw // 2, ZS), lax.rem(rw, 2)

    def device(xh=xh, y=y, xl=xl, z=z, c=c):
        return (xh * YS + y, xl * (2 * ZS) + z * 2 + c)

    y_right, y_left = lax.rem(y + 1, YS), lax.rem(y + YS - 1, YS)
    y_far = lax.rem(y + 2, YS)
    right, left = device(y=y_right), device(y=y_left)
    x_peer = device(xh=1 - xh)
    xl_peer = device(xl=1 - xl)
    partner = device(c=1 - c)
    z_up, z_down = device(z=lax.rem(z + 1, ZS)), device(z=lax.rem(z + ZS - 1, ZS))
    tm_peers = [(lax.rem(tm + i, 2 * YS), rw) for i in range(1, 2 * YS)]

    barrier = pltpu.get_barrier_semaphore()
    greeted = [partner, z_up, z_down, xl_peer, *tm_peers]
    for other in greeted:
        pl.semaphore_signal(barrier, inc=1, device_id=other, device_id_type=MESH)

    chunk = rows_dev // YS
    run = chunk // STREAMS // 2

    def rows_of(d, s, half=None):
        if half is None:
            return pl.ds(pl.multiple_of(d * chunk + s * 2 * run, run), 2 * run)
        return pl.ds(pl.multiple_of(d * chunk + (s * 2 + half) * run, run), run)

    order = [y_far, y_right, y_left, y]
    loads = []
    for i, d in enumerate(order):
        where = pl.ds(pl.multiple_of(d * chunk, chunk), chunk)
        load = pltpu.make_async_copy(record.at[:, where, :], rec.at[:, where, :], in_sem.at[i])
        load.start()
        loads.append(load)

    def send(src, dst, ssem, rsem, to):
        copy = pltpu.make_async_remote_copy(
            src, dst, ssem, rsem, device_id=to, device_id_type=MESH
        )
        copy.start()
        return copy

    sent = []

    lanes = iota((64, 128), 1)
    subs = iota((64, 128), 0)
    pattern_o = subs * C_A + lanes * C_B
    pattern_x = subs * C_B + lanes * C_A
    blocks = 2
    row0 = rw * rows_dev
    n_chunks = rows_dev // KC
    lhs = (lhs0, lhs1)

    def omega_hash(k):
        col0 = offsets[k] + tm * cols_dev
        for i in range(0, cols_dev, 64):
            base = pattern_o + ((col0 + i) * C_A + seeds[0] * C_S)
            omega[k * cols_dev + i : k * cols_dev + i + 64, :] = gauss(base, col_factor)

    def xi_hash(k):
        col0 = offsets[k] + tm * cols_dev
        for i in range(0, cols_dev, 64):
            for g in range(0, CORE, 128):
                base = pattern_x + ((col0 + i) * C_B + seeds[3] * C_S + wrapped(g * C_A))
                xit[k * cols_dev + i : k * cols_dev + i + 64, g : g + 128] = gauss(base, col_factor)

    def phi_ids():
        m = iota((CORE, 128), 0)
        mine = jnp.where(m >= HALF_PHI, 1, 0)
        m = m - mine * HALF_PHI
        owner_core = jnp.where(mine == 1, c, 1 - c)
        at_z = (m * 2731) >> 16
        rest = m - at_z * 24
        at_x = jnp.where(rest >= 12, 1, 0)
        row = (at_x * (2 * ZS) + at_z * 2 + owner_core) * 12 + (rest - at_x * 12)
        ids[...] = row * C_A + iota((CORE, 128), 1) * C_B + seeds[2] * C_S

    def psi_ids():
        m = iota((CORANGE, 128), 0)
        mine = m >> 7
        owner_core = jnp.where(mine == 1, c, 1 - c)
        row = ((m & 15) >> 3) * 128 + ((m & 127) >> 4) * 16 + owner_core * 8 + (m & 7)
        ids[0:CORANGE, :] = row * C_A + iota((CORANGE, 128), 1) * C_B + seeds[1] * C_S

    def hash_chunk(kc, rows):
        for g in range(0, KC, 128):
            shift = (row0 + (kc * KC + g)) * C_B
            for r in range(0, rows, 64):
                lhs[kc % 2][r : r + 64, g : g + 128] = gauss(ids[r : r + 64, :] + shift, row_factor)

    def dot_chunk(kc, rows, acc):
        for k in range(blocks):
            for n in range(0, cols_dev, 256):
                got = jnp.dot(
                    lhs[kc % 2][0:rows, :],
                    rec[k, kc * KC : (kc + 1) * KC, n : n + 256],
                    preferred_element_type=jnp.float32,
                )
                at = slice(k * cols_dev + n, k * cols_dev + n + 256)
                acc[:, at] = got if kc == 0 else acc[:, at] + got

    def core_dot(r0, rows):
        part_of = proj[r0 : r0 + rows, :]
        high = part_of.astype(jnp.bfloat16)
        low = (part_of - high.astype(jnp.float32)).astype(jnp.bfloat16)
        core[r0 : r0 + rows, :] = jnp.dot(
            high, xit[...], preferred_element_type=jnp.float32
        ) + jnp.dot(low, xit[...], preferred_element_type=jnp.float32)

    def range_chunk(d):
        where = pl.ds(pl.multiple_of(d * chunk, chunk), chunk)
        part[where, :] = jnp.dot(
            rec[0, where, :], omega[0:cols_dev, :], preferred_element_type=jnp.float32
        ) + jnp.dot(
            rec[1, where, :], omega[cols_dev : 2 * cols_dev, :], preferred_element_type=jnp.float32
        )

    S1, S2, S3, XC, G1, G2, Z, D = {}, {}, {}, {}, {}, {}, {}, {}

    def range_forward(s):
        S1[s, 0].wait_recv()
        fwd[s, 0] = part[rows_of(y_right, s, 0), :] + rb1[s, 0]
        S3[s, 0] = send(fwd.at[s, 0], rb3.at[s, 0], s3s.at[s, 0], s3r.at[s, 0], right)
        S1[s, 1].wait_recv()
        fwd[s, 1] = part[rows_of(y_left, s, 1), :] + rb1[s, 1]
        S3[s, 1] = send(fwd.at[s, 1], rb3.at[s, 1], s3s.at[s, 1], s3r.at[s, 1], left)

    def range_cross(s):
        S2[s, 0].wait_recv()
        S2[s, 1].wait_recv()
        S3[s, 0].wait_recv()
        S3[s, 1].wait_recv()
        ysum[s, 0:run] = part[rows_of(y, s, 0), :] + rb3[s, 0] + rb2[s, 1]
        ysum[s, run : 2 * run] = part[rows_of(y, s, 1), :] + rb2[s, 0] + rb3[s, 1]
        XC[s] = send(ysum.at[s], xb.at[s], xs.at[s], xr.at[s], x_peer)

    def range_spread(s):
        XC[s].wait_recv()
        own = rows_of(y, s)
        range_out[own, :] = ysum[s] + xb[s]
        G1[s, 0] = send(range_out.at[own], range_out.at[own], g1s.at[s, 0], g1r.at[s, 0], right)
        G1[s, 1] = send(range_out.at[own], range_out.at[own], g1s.at[s, 1], g1r.at[s, 1], left)

    def range_relay(s):
        G1[s, 0].wait_recv()
        a = rows_of(y_left, s, 0)
        G2[s, 0] = send(range_out.at[a], range_out.at[a], g2s.at[s, 0], g2r.at[s, 0], right)
        G1[s, 1].wait_recv()
        b = rows_of(y_right, s, 1)
        G2[s, 1] = send(range_out.at[b], range_out.at[b], g2s.at[s, 1], g2r.at[s, 1], left)

    def range_end(s):
        G2[s, 0].wait_recv()
        G2[s, 1].wait_recv()

    def z_step(what, step, up):
        d = lax.rem(z + (5 - step) if up else z + ZS - 5 + step, ZS)
        way = 0 if up else 1
        at = pl.ds(pl.multiple_of(d * (24 if what else 16), 8), 24 if what else 16)
        i = step - 1
        to = z_up if up else z_down
        if what:
            kept, got, sums, arrived = core.at[HALF_PHI:CORE], got_core, zs_core, zr_core
            pick = (slice(0, 16) if up else slice(16, 24), slice(None))
        else:
            kept, got, sums, arrived = cor.at[HALF_PSI:CORANGE], got_cor, zs_cor, zr_cor
            pick = (slice(None), slice(0, cols_dev) if up else slice(cols_dev, 2 * cols_dev))
        if step > 1:
            Z[what, step - 1, way].wait_recv()
        total = kept[at, :] + got[at, :]
        if step > 2:
            total = total + arrived[way, i - 1]
        sums[way, i] = total
        if step == 2:
            sums[(way, i, *pick)] += arrived[(way, 0, *pick)]
        pick = (way, i, *pick) if step == 1 else (way, i)
        Z[what, step, way] = send(
            sums.at[pick], arrived.at[pick], zs.at[way, i, what], zr.at[way, i, what], to
        )

    def pair(what, src, dst):
        D[what] = send(src, dst, ds.at[what], dr.at[what], partner)

    phi_ids()
    hash_chunk(0, CORE)
    for load in loads:
        load.wait()
    for kc in range(n_chunks):
        if kc + 1 < n_chunks:
            hash_chunk(kc + 1, CORE)
        else:
            xi_hash(0)
            xi_hash(1)
        dot_chunk(kc, CORE, proj)
    core_dot(0, HALF_PHI)
    pl.semaphore_wait(barrier, len(greeted))
    pair(1, core.at[0:HALF_PHI], got_core)
    core_dot(HALF_PHI, HALF_PHI)
    omega_hash(0)
    omega_hash(1)

    range_chunk(y_far)
    for s in range(STREAMS):
        S1[s, 0] = send(part.at[rows_of(y_far, s, 0)], rb1.at[s, 0], s1s.at[s, 0], s1r.at[s, 0], right)
        S1[s, 1] = send(part.at[rows_of(y_far, s, 1)], rb1.at[s, 1], s1s.at[s, 1], s1r.at[s, 1], left)
    D[1].wait_recv()
    z_step(1, 1, True)
    z_step(1, 1, False)
    psi_ids()
    hash_chunk(0, CORANGE)
    range_chunk(y_right)
    range_chunk(y_left)
    for s in range(STREAMS):
        S2[s, 0] = send(part.at[rows_of(y_right, s, 1)], rb2.at[s, 0], s2s.at[s, 0], s2r.at[s, 0], right)
        S2[s, 1] = send(part.at[rows_of(y_left, s, 0)], rb2.at[s, 1], s2s.at[s, 1], s2r.at[s, 1], left)
    hash_chunk(1, CORANGE)
    dot_chunk(0, CORANGE, cor)
    range_chunk(y)
    z_step(1, 2, True)
    z_step(1, 2, False)
    hash_chunk(2, CORANGE)
    dot_chunk(1, CORANGE, cor)
    range_forward(0)
    hash_chunk(3, CORANGE)
    dot_chunk(2, CORANGE, cor)
    dot_chunk(3, CORANGE, cor)
    pair(0, cor.at[0:HALF_PSI], got_cor)
    for s in range(1, STREAMS):
        range_forward(s)
    z_step(1, 3, True)
    z_step(1, 3, False)
    D[0].wait_recv()
    z_step(0, 1, True)
    z_step(0, 1, False)
    range_cross(0)
    z_step(1, 4, True)
    z_step(1, 4, False)
    for s in range(1, STREAMS):
        range_cross(s)
    z_step(0, 2, True)
    z_step(0, 2, False)
    own_cor = pl.ds(pl.multiple_of(HALF_PSI + z * 16, 16), 16)
    own_core = pl.ds(pl.multiple_of(HALF_PHI + z * 24, 8), 24)
    core[own_core, :] += got_core[pl.ds(pl.multiple_of(z * 24, 8), 24), :]
    cor[own_cor, :] += got_cor[pl.ds(pl.multiple_of(z * 16, 16), 16), :]
    range_spread(0)
    Z[1, 4, 0].wait_recv()
    Z[1, 4, 1].wait_recv()
    core[own_core, :] += zr_core[0, 3] + zr_core[1, 3]
    L1 = send(core.at[own_core], xl_core, ls.at[1], lr.at[1], xl_peer)
    for s in range(1, STREAMS):
        range_spread(s)
    z_step(0, 3, True)
    z_step(0, 3, False)
    range_relay(0)
    L1.wait_recv()
    both = core[own_core, :] + xl_core[...]
    tmb[tm, 0:12, :] = jnp.where(xl == 0, both[0:12, :], both[12:24, :])
    tmb[tm, 12:16, :] = jnp.zeros((4, CORE), jnp.float32)
    T = [
        send(tmb.at[tm], tmb.at[tm], ts.at[i], tr.at[i], to) for i, to in enumerate(tm_peers)
    ]
    for s in range(1, STREAMS):
        range_relay(s)
    z_step(0, 4, True)
    z_step(0, 4, False)
    Z[0, 4, 0].wait_recv()
    Z[0, 4, 1].wait_recv()
    cor[own_cor, :] += zr_cor[0, 3] + zr_cor[1, 3]
    other = pl.ds(pl.multiple_of(HALF_PSI + z * 16 + (1 - xl) * 8, 8), 8)
    L0 = send(cor.at[other], xl_cor, ls.at[0], lr.at[0], xl_peer)
    for copy in T:
        copy.wait_recv()
    total = tmb[0, 0:12, :]
    for i in range(1, 2 * YS):
        total = total + tmb[i, 0:12, :]
    core_out[...] = total
    for s in range(STREAMS):
        range_end(s)
    L0.wait_recv()
    mine = cor[pl.ds(pl.multiple_of(HALF_PSI + z * 16 + xl * 8, 8), 8), :] + xl_cor[...]
    for k in range(blocks):
        corange_out[k] = mine[:, k * cols_dev : (k + 1) * cols_dev]
    for group in (S1, S2, S3, XC, G1, G2, Z, D):
        for copy in group.values():
            copy.wait_send()
    for copy in [L0, L1, *T]:
        copy.wait_send()


def shards(record, seed_list, block_offsets):
    blocks, rows_dev, cols_dev = record.shape
    rows_count, time_count = lax.axis_size("rows"), lax.axis_size("tm")
    row_factor = 1.0 / (147.8 * math.sqrt(rows_dev * rows_count))
    col_factor = 1.0 / (147.8 * math.sqrt(blocks * cols_dev * time_count))
    run = rows_dev // YS // STREAMS // 2
    f32, bf16 = jnp.float32, jnp.bfloat16
    vmem, dma = pltpu.VMEM, pltpu.SemaphoreType.DMA
    shapes = (
        (rows_dev, RANGE),
        (blocks, CORANGE // rows_count, cols_dev),
        (CORE // rows_count, CORE),
    )
    held = pl.pallas_call(
        functools.partial(kernel, row_factor, col_factor, rows_dev, cols_dev),
        out_shape=tuple(pltpu.VMEM(shape, f32) for shape in shapes),
        in_specs=[
            pl.BlockSpec(memory_space=pltpu.SMEM),
            pl.BlockSpec(memory_space=pltpu.SMEM),
            pl.BlockSpec(memory_space=pl.ANY),
        ],
        out_specs=(pl.BlockSpec(memory_space=pltpu.VMEM),) * 3,
        scratch_shapes=[
            vmem((blocks, rows_dev, cols_dev), bf16),
            vmem((blocks * cols_dev, RANGE), bf16),
            vmem((blocks * cols_dev, CORE), bf16),
            vmem((CORE, 128), jnp.int32),
            vmem((CORE, KC), bf16),
            vmem((CORE, KC), bf16),
            vmem((CORE, blocks * cols_dev), f32),
            vmem((CORANGE, blocks * cols_dev), f32),
            vmem((CORE, CORE), f32),
            vmem((rows_dev, RANGE), f32),
            vmem((STREAMS, 2, run, RANGE), f32),
            vmem((STREAMS, 2, run, RANGE), f32),
            vmem((STREAMS, 2, run, RANGE), f32),
            vmem((STREAMS, 2, run, RANGE), f32),
            vmem((STREAMS, 2 * run, RANGE), f32),
            vmem((STREAMS, 2 * run, RANGE), f32),
            vmem((HALF_PSI, blocks * cols_dev), f32),
            vmem((HALF_PHI, CORE), f32),
            vmem((2, 4, 16, blocks * cols_dev), f32),
            vmem((2, 4, 24, CORE), f32),
            vmem((2, 4, 16, blocks * cols_dev), f32),
            vmem((2, 4, 24, CORE), f32),
            vmem((8, blocks * cols_dev), f32),
            vmem((24, CORE), f32),
            vmem((2 * YS, 16, CORE), f32),
            dma((YS,)),
            *[dma((STREAMS, 2))] * 6,
            *[dma((STREAMS,))] * 2,
            *[dma((STREAMS, 2))] * 4,
            *[dma((2,))] * 2,
            *[dma((2, 4, 2))] * 2,
            *[dma((2,))] * 2,
            *[dma((2 * YS - 1,))] * 2,
        ],
        compiler_params=pltpu.CompilerParams(collective_id=0, has_side_effects=True),
        name="three_sketch",
    )(seed_list, block_offsets, record)
    return held


def solution(mesh):
    placed = (P(None, "rows", "tm"), P(), P())
    return jax.shard_map(
        shards,
        mesh=mesh,
        in_specs=placed,
        out_specs=(P("rows", None), P(None, "rows", "tm"), P("rows", None)),
        check_vma=False,
    )
```

time: 56.5 us -> 49.4 us (0.87)
  the two profiles are of different devices: /device:TPU:32 before, /device:TPU:10 now
where the time goes in v2:
time: 49.4 us
  Pallas kernels  46.5 us (94%)
  local copies, waits for them, and re-layouts  2.19 us (4%)
  between operations  0.64 us (1%)
    pallas_call x1, Pallas kernels, shards(): pl.pallas_call(functools.partial(kernel, row_factor, col_factor, rows_dev...  46.5 us
    unnamed x3, local copies, waits for them, and re-layouts  2.19 us

profile of v2, /device:TPU:10, one launch (start us, length us, event | category | flops | bytes accessed | tf_op | source)
XLA Modules:
  0.0 49.4 jit_solution(5232707769864849745)
XLA Ops:
  0.6 46.5 %three_sketch.1 = (f32[2048,128]{1,0:T(8,128)S(1)}, f32[2,8,512]{2,1,0:T(8,128)S(1)}, f32[12,384]{1,0:T(8,128)S(1)}) custom-call(s32[4]{0:T(128)} %seeds.1, s32[2]{0:T(128)} %offsets.1, bf16[2,2048,512]{2,1,0:T(8,128)(2,1)} %record.1), custom_call_target="tpu_custom_call" | custom-call | tf_op jit(solution)/shard_map/three_sketch/pallas_call | solution.py:365
  47.2 1.0 %copy.9 = f32[2048,128]{1,0:T(8,128)} copy(f32[2048,128]{1,0:T(8,128)S(1)} %get-tuple-element.3) | data formatting | bytes 2097152
  48.1 0.6 %copy.11 = f32[12,384]{1,0:T(8,128)} copy(f32[12,384]{1,0:T(8,128)S(1)} %get-tuple-element.5) | data formatting | bytes 36864
  48.7 0.6 %copy.10 = f32[2,8,512]{2,1,0:T(8,128)} copy(f32[2,8,512]{2,1,0:T(8,128)S(1)} %get-tuple-element.4) | data formatting | bytes 65536

commit v3 on v2

v3 whole, which is shorter than its diff:
```python
import functools
import math

import jax
import jax.numpy as jnp
from jax import lax
from jax.experimental import pallas as pl
from jax.experimental.pallas import tpu as pltpu
from jax.sharding import PartitionSpec as P

RANGE = 128
CORANGE = 256
CORE = 384
C_A = 668265263
C_B = 374761393
C_S = 625341585
MESH = pl.DeviceIdType.MESH

YS = 4
ZS = 8
STREAMS = 4
HALF_PSI = CORANGE // 2
HALF_PHI = CORE // 2
KC = 512


def srl(values, amount):
    return lax.shift_right_logical(values, jnp.full(values.shape, amount, jnp.int32))


def gauss(base, factor):
    h = base ^ srl(base, 15)
    h = h * 739982445
    h = h ^ srl(h, 12)
    h = h * 695872825
    h = h ^ srl(h, 15)
    pairs = (h & 0x00FF00FF) + (srl(h, 8) & 0x00FF00FF)
    total = (pairs + srl(pairs, 16)) & 0x7FF
    return ((total - 510).astype(jnp.float32) * factor).astype(jnp.bfloat16)


def wrapped(number):
    return (number + (1 << 31)) % (1 << 32) - (1 << 31)


def iota(shape, dim):
    return lax.broadcasted_iota(jnp.int32, shape, dim)


def kernel(
    row_factor, col_factor, rows_dev, cols_dev,
    seeds_in, offsets_in, record,
    range_out, corange_out, core_out,
    seeds, offsets, rec, omega, xit, phi_ids, psi_ids, phi_lhs0, phi_lhs1, psi_lhs, proj, cor, core,
    part, rb0, rb1, rb2, fwd, ysum, xb,
    got_cor, got_core, zr_cor, zr_core, zs_cor, zs_core, xl_cor, shares, xg, yg,
    in_sem, out_sem, s1r, cr, xr, g1r, g2r, dr, zr, lr, tr, ur,
):
    tm, rw = lax.axis_index("tm"), lax.axis_index("rows")
    xh, y = tm // YS, lax.rem(tm, YS)
    xl, z, c = rw // (2 * ZS), lax.rem(rw // 2, ZS), lax.rem(rw, 2)

    def device(xh=xh, y=y, xl=xl, z=z, c=c):
        return (xh * YS + y, xl * (2 * ZS) + z * 2 + c)

    y_right, y_left = lax.rem(y + 1, YS), lax.rem(y + YS - 1, YS)
    y_far = lax.rem(y + 2, YS)
    right, left = device(y=y_right), device(y=y_left)
    x_peer = device(xh=1 - xh)
    xl_peer = device(xl=1 - xl)
    partner = device(c=1 - c)
    z_up, z_down = device(z=lax.rem(z + 1, ZS)), device(z=lax.rem(z + ZS - 1, ZS))
    far = device(y=y_far)
    xx_peer = device(xh=1 - xh, xl=1 - xl)

    scalars = [
        pltpu.make_async_copy(seeds_in, seeds, in_sem.at[YS]),
        pltpu.make_async_copy(offsets_in, offsets, in_sem.at[YS + 1]),
    ]
    for load in scalars:
        load.start()
    chunk = rows_dev // YS
    order = [y_far, y_right, y_left, y]
    loads = []
    for i, d in enumerate(order):
        where = pl.ds(pl.multiple_of(d * chunk, chunk), chunk)
        load = pltpu.make_async_copy(record.at[:, where, :], rec.at[:, where, :], in_sem.at[i])
        load.start()
        loads.append(load)

    barrier = pltpu.get_barrier_semaphore()
    greeted = [partner, z_up, z_down, xl_peer, x_peer, xx_peer, right, left, far]
    for other in greeted:
        pl.semaphore_signal(barrier, inc=1, device_id=other, device_id_type=MESH)

    run = chunk // STREAMS // 2

    def rows_of(d, s, half=None):
        if half is None:
            return pl.ds(pl.multiple_of(d * chunk + s * 2 * run, run), 2 * run)
        return pl.ds(pl.multiple_of(d * chunk + (s * 2 + half) * run, run), run)

    sent = [0, 0, 0]

    def send(group, src, dst, rsem, to):
        sent[group] += math.prod(src.shape) * 4
        copy = pltpu.make_async_remote_copy(
            src, dst, out_sem.at[group], rsem, device_id=to, device_id_type=MESH
        )
        copy.start()
        return copy

    def arrive(like, rsem):
        pltpu.make_async_copy(like, like, rsem).wait()

    lanes = iota((64, 128), 1)
    subs = iota((64, 128), 0)
    pattern_o = subs * C_A + lanes * C_B
    pattern_x = subs * C_B + lanes * C_A
    blocks = 2
    row0 = rw * rows_dev
    n_chunks = rows_dev // KC

    def omega_hash(k):
        col0 = offsets[k] + tm * cols_dev
        for i in range(0, cols_dev, 64):
            base = pattern_o + ((col0 + i) * C_A + seeds[0] * C_S)
            omega[k * cols_dev + i : k * cols_dev + i + 64, :] = gauss(base, col_factor)

    def xi_hash(k):
        col0 = offsets[k] + tm * cols_dev
        for i in range(0, cols_dev, 64):
            for g in range(0, CORE, 128):
                base = pattern_x + ((col0 + i) * C_B + seeds[3] * C_S + wrapped(g * C_A))
                xit[k * cols_dev + i : k * cols_dev + i + 64, g : g + 128] = gauss(base, col_factor)

    def make_ids():
        m = iota((CORE, 128), 0)
        mine = jnp.where(m >= HALF_PHI, 1, 0)
        m = m - mine * HALF_PHI
        owner_core = jnp.where(mine == 1, c, 1 - c)
        at_z = (m * 2731) >> 16
        rest = m - at_z * 24
        at_x = jnp.where(rest >= 12, 1, 0)
        row = (at_x * (2 * ZS) + at_z * 2 + owner_core) * 12 + (rest - at_x * 12)
        phi_ids[...] = row * C_A + iota((CORE, 128), 1) * C_B
        m = iota((CORANGE, 128), 0)
        owner_core = jnp.where(m >= HALF_PSI, c, 1 - c)
        row = ((m & 15) >> 3) * 128 + ((m & 127) >> 4) * 16 + owner_core * 8 + (m & 7)
        psi_ids[...] = row * C_A + iota((CORANGE, 128), 1) * C_B

    def row_hash(kc, ids, lhs, seed):
        for g in range(0, KC, 128):
            shift = (row0 + (kc * KC + g)) * C_B + seed * C_S
            for r in range(0, ids.shape[0], 64):
                lhs[r : r + 64, g : g + 128] = gauss(ids[r : r + 64, :] + shift, row_factor)

    def phi_hash(kc):
        row_hash(kc, phi_ids, (phi_lhs0, phi_lhs1)[kc % 2], seeds[2])

    def psi_hash(kc):
        row_hash(kc, psi_ids, psi_lhs.at[:, kc * KC : (kc + 1) * KC], seeds[1])

    def phi_dot(kc):
        for k in range(blocks):
            for n in range(0, cols_dev, 256):
                got = jnp.dot(
                    (phi_lhs0, phi_lhs1)[kc % 2][...],
                    rec[k, kc * KC : (kc + 1) * KC, n : n + 256],
                    preferred_element_type=jnp.float32,
                )
                at = slice(k * cols_dev + n, k * cols_dev + n + 256)
                proj[:, at] = got if kc == 0 else proj[:, at] + got

    def psi_dot(k):
        for n in range(0, cols_dev, 256):
            cor[:, k * cols_dev + n : k * cols_dev + n + 256] = jnp.dot(
                psi_lhs[...], rec[k, :, n : n + 256], preferred_element_type=jnp.float32
            )

    def core_dot(r0, rows):
        part_of = proj[r0 : r0 + rows, :]
        high = part_of.astype(jnp.bfloat16)
        low = (part_of - high.astype(jnp.float32)).astype(jnp.bfloat16)
        core[r0 : r0 + rows, :] = jnp.dot(
            high, xit[...], preferred_element_type=jnp.float32
        ) + jnp.dot(low, xit[...], preferred_element_type=jnp.float32)

    def range_chunk(d):
        where = pl.ds(pl.multiple_of(d * chunk, chunk), chunk)
        part[where, :] = jnp.dot(
            rec[0, where, :], omega[0:cols_dev, :], preferred_element_type=jnp.float32
        ) + jnp.dot(
            rec[1, where, :], omega[cols_dev : 2 * cols_dev, :], preferred_element_type=jnp.float32
        )

    Z, D = {}, {}

    def range_forward(s):
        arrive(rb1.at[s], s1r.at[s])
        fwd[s, 0] = part[rows_of(y_right, s, 0), :] + rb1[s, 0]
        send(0, fwd.at[s, 0], rb2.at[s, 2], cr.at[s], right)
        fwd[s, 1] = part[rows_of(y_left, s, 1), :] + rb1[s, 1]
        send(0, fwd.at[s, 1], rb2.at[s, 3], cr.at[s], left)

    def range_cross(s):
        if s == 0:
            arrive(rb0, cr.at[0])
            ysum[0] = part[rows_of(y, 0), :] + rb0[0] + (rb0[1] + rb0[2])
        else:
            arrive(rb2.at[s], cr.at[s])
            ysum[s, 0:run] = part[rows_of(y, s, 0), :] + rb2[s, 2] + rb2[s, 1]
            ysum[s, run : 2 * run] = part[rows_of(y, s, 1), :] + rb2[s, 0] + rb2[s, 3]
        send(0, ysum.at[s], xb.at[s], xr.at[s], x_peer)

    def range_spread(s):
        arrive(xb.at[s], xr.at[s])
        own = rows_of(y, s)
        range_out[own, :] = ysum[s] + xb[s]
        last = s == STREAMS - 1
        if last:
            send(0, range_out.at[own], range_out.at[own], g2r.at[0], far)
        sem = g2r.at[0] if last else g1r.at[s]
        send(0, range_out.at[own], range_out.at[own], sem, right)
        send(0, range_out.at[own], range_out.at[own], sem, left)

    def range_relay(s):
        arrive(range_out.at[0 : 4 * run], g1r.at[s])
        a = rows_of(y_left, s, 0)
        send(0, range_out.at[a], range_out.at[a], g2r.at[0], right)
        b = rows_of(y_right, s, 1)
        send(0, range_out.at[b], range_out.at[b], g2r.at[0], left)

    def range_end():
        arrive(range_out.at[0 : (2 * (STREAMS - 1) + 6) * run], g2r.at[0])

    def z_step(what, step, up):
        d = lax.rem(z + (5 - step) if up else z + ZS - 5 + step, ZS)
        way = 0 if up else 1
        at = pl.ds(pl.multiple_of(d * (24 if what else 16), 8), 24 if what else 16)
        i = step - 1
        to = z_up if up else z_down
        if what:
            kept, got, sums, arrived = core.at[HALF_PHI:CORE], got_core, zs_core, zr_core
            pick = (slice(0, 16) if up else slice(16, 24), slice(None))
        else:
            kept, got, sums, arrived = cor.at[HALF_PSI:CORANGE], got_cor, zs_cor, zr_cor
            pick = (slice(None), slice(0, cols_dev) if up else slice(cols_dev, 2 * cols_dev))
        if step == 1:
            rows, cols = pick
            at = pl.ds(pl.multiple_of(d * 24 + rows.start, 8), rows.stop - rows.start) if what else at
            sums[(way, 0, *pick)] = kept[at, cols] + got[at, cols]
        else:
            Z[what, step - 1, way].wait_recv()
            total = kept[at, :] + got[at, :]
            if step > 2:
                total = total + arrived[way, i - 1]
            sums[way, i] = total
            if step == 2:
                sums[(way, i, *pick)] += arrived[(way, 0, *pick)]
        pick = (way, i, *pick) if step == 1 else (way, i)
        sem = zr.at[what, 6 if step == 4 else 3 * way + i]
        Z[what, step, way] = send(1, sums.at[pick], arrived.at[pick], sem, to)

    def pair(what, src, dst):
        D[what] = send(2, src, dst, dr.at[what], partner)

    make_ids()
    for load in scalars:
        load.wait()
    omega_hash(0)
    omega_hash(1)
    xi_hash(0)
    loads[0].wait()
    range_chunk(y_far)
    xi_hash(1)
    pl.semaphore_wait(barrier, len(greeted))
    send(0, part.at[rows_of(y_far, 0)], rb0.at[0], cr.at[0], far)
    for s in range(1, STREAMS):
        send(0, part.at[rows_of(y_far, s, 0)], rb1.at[s, 0], s1r.at[s], right)
        send(0, part.at[rows_of(y_far, s, 1)], rb1.at[s, 1], s1r.at[s], left)
    for load in loads[1:]:
        load.wait()
    phi_hash(0)
    range_chunk(y_right)
    range_chunk(y_left)
    send(0, part.at[rows_of(y_right, 0)], rb0.at[1], cr.at[0], right)
    send(0, part.at[rows_of(y_left, 0)], rb0.at[2], cr.at[0], left)
    for s in range(1, STREAMS):
        send(0, part.at[rows_of(y_right, s, 1)], rb2.at[s, 0], cr.at[s], right)
        send(0, part.at[rows_of(y_left, s, 0)], rb2.at[s, 1], cr.at[s], left)
    phi_hash(1)
    phi_dot(0)
    phi_hash(2)
    phi_dot(1)
    phi_hash(3)
    phi_dot(2)
    psi_hash(0)
    phi_dot(3)
    core_dot(0, HALF_PHI)
    pair(2, core.at[0:HALF_PHI], got_core)
    range_forward(1)
    range_chunk(y)
    psi_hash(1)
    core_dot(HALF_PHI, HALF_PHI)
    psi_hash(2)
    range_forward(2)
    range_forward(3)
    psi_hash(3)
    range_cross(0)
    D[2].wait_recv()
    z_step(1, 1, True)
    z_step(1, 1, False)
    psi_dot(0)
    pair(0, cor.at[0:HALF_PSI, 0:cols_dev], got_cor.at[:, 0:cols_dev])
    psi_dot(1)
    pair(1, cor.at[0:HALF_PSI, cols_dev : 2 * cols_dev], got_cor.at[:, cols_dev : 2 * cols_dev])
    D[0].wait_recv()
    z_step(0, 1, True)
    D[1].wait_recv()
    z_step(0, 1, False)
    z_step(1, 2, True)
    z_step(1, 2, False)
    range_cross(1)
    range_cross(2)
    range_spread(0)
    range_cross(3)
    z_step(0, 2, True)
    z_step(0, 2, False)
    z_step(1, 3, True)
    z_step(1, 3, False)
    own_cor = pl.ds(pl.multiple_of(HALF_PSI + z * 16, 16), 16)
    own_core = pl.ds(pl.multiple_of(HALF_PHI + z * 24, 8), 24)
    core[own_core, :] += got_core[pl.ds(pl.multiple_of(z * 24, 8), 24), :]
    cor[own_cor, :] += got_cor[pl.ds(pl.multiple_of(z * 16, 16), 16), :]
    range_spread(1)
    z_step(0, 3, True)
    z_step(0, 3, False)
    range_relay(0)
    range_spread(2)
    z_step(1, 4, True)
    z_step(1, 4, False)
    range_spread(3)
    z_step(0, 4, True)
    z_step(0, 4, False)
    arrive(zr_core.at[0:2, 3], zr.at[1, 6])
    both = core[own_core, :] + zr_core[0, 3] + zr_core[1, 3]
    pad = jnp.zeros((4, CORE), jnp.float32)
    for i in range(2):
        shares[i, 0:12, :] = both[i * 12 : i * 12 + 12, :]
        shares[i, 12:16, :] = pad
    me_x = xh * 2 + xl
    send(2, shares.at[1 - xl], xg.at[me_x], tr.at[0], xl_peer)
    send(2, shares.at[xl], xg.at[me_x], tr.at[0], x_peer)
    send(2, shares.at[1 - xl], xg.at[me_x], tr.at[0], xx_peer)
    xg[me_x] = shares[xl]
    range_relay(1)
    arrive(xg.at[0:3], tr.at[0])
    yg[y] = (xg[0] + xg[1]) + (xg[2] + xg[3])
    for to in (right, left, far):
        send(2, yg.at[y], yg.at[y], ur.at[0], to)
    arrive(zr_cor.at[0:2, 3], zr.at[0, 6])
    cor[own_cor, :] += zr_cor[0, 3] + zr_cor[1, 3]
    other = pl.ds(pl.multiple_of(HALF_PSI + z * 16 + (1 - xl) * 8, 8), 8)
    send(2, cor.at[other], xl_cor, lr.at[0], xl_peer)
    range_relay(2)
    arrive(xl_cor, lr.at[0])
    mine = cor[pl.ds(pl.multiple_of(HALF_PSI + z * 16 + xl * 8, 8), 8), :] + xl_cor[...]
    for k in range(blocks):
        corange_out[k] = mine[:, k * cols_dev : (k + 1) * cols_dev]
    arrive(yg.at[0:3], ur.at[0])
    total = (yg[0] + yg[1]) + (yg[2] + yg[3])
    core_out[...] = total[0:12, :]
    range_end()
    for group, ref in enumerate((rec, part, rec)):
        rows = sent[group] // (ref.shape[-1] * ref.dtype.itemsize)
        view = ref.at[0, 0:rows] if ref is rec else ref.at[0:rows]
        arrive(view, out_sem.at[group])


def put_out(*refs):
    copies = [pltpu.make_async_copy(refs[i], refs[3 + i], refs[6].at[i]) for i in range(3)]
    for copy in copies:
        copy.start()
    for copy in copies:
        copy.wait()


def shards(record, seed_list, block_offsets):
    blocks, rows_dev, cols_dev = record.shape
    rows_count, time_count = lax.axis_size("rows"), lax.axis_size("tm")
    row_factor = 1.0 / (147.8 * math.sqrt(rows_dev * rows_count))
    col_factor = 1.0 / (147.8 * math.sqrt(blocks * cols_dev * time_count))
    run = rows_dev // YS // STREAMS // 2
    f32, bf16 = jnp.float32, jnp.bfloat16
    vmem, dma = pltpu.VMEM, pltpu.SemaphoreType.DMA
    shapes = (
        (rows_dev, RANGE),
        (blocks, CORANGE // rows_count, cols_dev),
        (CORE // rows_count, CORE),
    )
    held = pl.pallas_call(
        functools.partial(kernel, row_factor, col_factor, rows_dev, cols_dev),
        out_shape=tuple(pltpu.VMEM(shape, f32) for shape in shapes),
        in_specs=[
            pl.BlockSpec(memory_space=pl.ANY),
            pl.BlockSpec(memory_space=pl.ANY),
            pl.BlockSpec(memory_space=pl.ANY),
        ],
        out_specs=(pl.BlockSpec(memory_space=pltpu.VMEM),) * 3,
        scratch_shapes=[
            pltpu.SMEM((4,), jnp.int32),
            pltpu.SMEM((blocks,), jnp.int32),
            vmem((blocks, rows_dev, cols_dev), bf16),
            vmem((blocks * cols_dev, RANGE), bf16),
            vmem((blocks * cols_dev, CORE), bf16),
            vmem((CORE, 128), jnp.int32),
            vmem((CORANGE, 128), jnp.int32),
            vmem((CORE, KC), bf16),
            vmem((CORE, KC), bf16),
            vmem((CORANGE, rows_dev), bf16),
            vmem((CORE, blocks * cols_dev), f32),
            vmem((CORANGE, blocks * cols_dev), f32),
            vmem((CORE, CORE), f32),
            vmem((rows_dev, RANGE), f32),
            vmem((3, 2 * run, RANGE), f32),
            vmem((STREAMS, 2, run, RANGE), f32),
            vmem((STREAMS, 4, run, RANGE), f32),
            vmem((STREAMS, 2, run, RANGE), f32),
            vmem((STREAMS, 2 * run, RANGE), f32),
            vmem((STREAMS, 2 * run, RANGE), f32),
            vmem((HALF_PSI, blocks * cols_dev), f32),
            vmem((HALF_PHI, CORE), f32),
            vmem((2, 4, 16, blocks * cols_dev), f32),
            vmem((2, 4, 24, CORE), f32),
            vmem((2, 4, 16, blocks * cols_dev), f32),
            vmem((2, 4, 24, CORE), f32),
            vmem((8, blocks * cols_dev), f32),
            vmem((2, 16, CORE), f32),
            vmem((4, 16, CORE), f32),
            vmem((YS, 16, CORE), f32),
            dma((YS + 2,)),
            dma((3,)),
            dma((STREAMS,)),
            dma((STREAMS,)),
            dma((STREAMS,)),
            dma((STREAMS - 1,)),
            dma((1,)),
            dma((3,)),
            dma((2, 7)),
            dma((1,)),
            dma((1,)),
            dma((1,)),
        ],
        compiler_params=pltpu.CompilerParams(collective_id=0, has_side_effects=True),
        name="three_sketch",
    )(seed_list, block_offsets, record)
    return pl.pallas_call(
        put_out,
        out_shape=tuple(jax.ShapeDtypeStruct(shape, f32) for shape in shapes),
        in_specs=[pl.BlockSpec(memory_space=pltpu.VMEM)] * 3,
        out_specs=(pl.BlockSpec(memory_space=pl.ANY),) * 3,
        scratch_shapes=[dma((3,))],
        name="put_out",
    )(*[pltpu.with_memory_space_constraint(x, pltpu.VMEM) for x in held])


def solution(mesh):
    placed = (P(None, "rows", "tm"), P(), P())
    return jax.shard_map(
        shards,
        mesh=mesh,
        in_specs=placed,
        out_specs=(P("rows", None), P(None, "rows", "tm"), P("rows", None)),
        check_vma=False,
    )
```

time: 49.4 us -> 40 us (0.81)
  the two profiles are of different devices: /device:TPU:10 before, /device:TPU:32 now
where the time goes in v3:
time: 40 us; the launch traced here: 39.7 us
  Pallas kernels  39.1 us (98%)
  between operations  0.64 us (2%)
    pallas_call x1, Pallas kernels, shards(): pl.pallas_call(functools.partial(kernel, row_factor, col_factor, rows_dev...  38.1 us
    pallas_call x1, Pallas kernels, shards(): pl.pallas_call(put_out, out_shape=tuple((jax.ShapeDtypeStruct(shape, f32)...  1 us

profile of v3, /device:TPU:32, one launch (start us, length us, event | category | flops | bytes accessed | tf_op | source)
XLA Modules:
  0.0 39.7 jit_solution(4210807812633033881)
XLA Ops:
  0.6 38.1 %three_sketch.1 = (f32[2048,128]{1,0:T(8,128)S(1)}, f32[2,8,512]{2,1,0:T(8,128)S(1)}, f32[12,384]{1,0:T(8,128)S(1)}) custom-call(s32[4]{0:T(128)} %seeds_in.1, s32[2]{0:T(128)} %offsets_in.1, bf16[2,2048,512]{2,1,0:T(8,128)(2,1)} %record.1), custom_call_target="tpu_custom_call" | custom-call | tf_op jit(solution)/shard_map/three_sketch/pallas_call | solution.py:402
  38.7 1.0 %put_out.1 = (f32[2048,128]{1,0:T(8,128)}, f32[2,8,512]{2,1,0:T(8,128)}, f32[12,384]{1,0:T(8,128)}) custom-call(f32[2048,128]{1,0:T(8,128)S(1)} %get-tuple-element.6.refs_0_, f32[2,8,512]{2,1,0:T(8,128)S(1)} %get-tuple-element.7.refs_1_, f32[12,384]{1,0:T(8,128)S(1)} %get-tuple-element.8.refs_2_), custom_call_target="tpu_custom_call" | custom-call | tf_op jit(solution)/shard_map/put_out/pallas_call | solution.py:458

commit v4 on v3

--- a/solution.py
+++ b/solution.py
@@ -35,7 +35,7 @@
     h = h * 695872825
     h = h ^ srl(h, 15)
     pairs = (h & 0x00FF00FF) + (srl(h, 8) & 0x00FF00FF)
-    total = (pairs + srl(pairs, 16)) & 0x7FF
+    total = srl(pairs * 0x00010001, 16)
     return ((total - 510).astype(jnp.float32) * factor).astype(jnp.bfloat16)
 
 
@@ -53,8 +53,8 @@
     range_out, corange_out, core_out,
     seeds, offsets, rec, omega, xit, phi_ids, psi_ids, phi_lhs0, phi_lhs1, psi_lhs, proj, cor, core,
     part, rb0, rb1, rb2, fwd, ysum, xb,
-    got_cor, got_core, zr_cor, zr_core, zs_cor, zs_core, xl_cor, shares, xg, yg,
-    in_sem, out_sem, s1r, cr, xr, g1r, g2r, dr, zr, lr, tr, ur,
+    got_cor, got_core, zr_cor, zr_core, zs_cor, zs_core, zs_own, fin, shares, xg, yg,
+    in_sem, out_sem, s1r, cr, xr, g1r, g2r, dr, zr, fr, kr, tr, ur,
 ):
     tm, rw = lax.axis_index("tm"), lax.axis_index("rows")
     xh, y = tm // YS, lax.rem(tm, YS)
@@ -66,6 +66,8 @@
     y_right, y_left = lax.rem(y + 1, YS), lax.rem(y + YS - 1, YS)
     y_far = lax.rem(y + 2, YS)
     right, left = device(y=y_right), device(y=y_left)
+    z_up_x, z_down_x = device(z=lax.rem(z + 1, ZS), xl=1 - xl), device(z=lax.rem(z + ZS - 1, ZS), xl=1 - xl)
+    z_up3, z_down3 = device(z=lax.rem(z + 3, ZS)), device(z=lax.rem(z + ZS - 3, ZS))
     x_peer = device(xh=1 - xh)
     xl_peer = device(xl=1 - xl)
     partner = device(c=1 - c)
@@ -89,7 +91,7 @@
         loads.append(load)
 
     barrier = pltpu.get_barrier_semaphore()
-    greeted = [partner, z_up, z_down, xl_peer, x_peer, xx_peer, right, left, far]
+    greeted = [partner, z_up, z_down, z_up3, z_down3, z_up_x, z_down_x, xl_peer, x_peer, xx_peer, right, left, far]
     for other in greeted:
         pl.semaphore_signal(barrier, inc=1, device_id=other, device_id_type=MESH)
 
@@ -121,18 +123,36 @@
     row0 = rw * rows_dev
     n_chunks = rows_dev // KC
 
+    def together(matrix, vector):
+        done = 0
+        for i, piece in enumerate(matrix):
+            piece()
+            until = (i + 1) * len(vector) // len(matrix)
+            for other in vector[done:until]:
+                other()
+            done = until
+
+    def run_all(pieces):
+        for piece in pieces:
+            piece()
+
     def omega_hash(k):
         col0 = offsets[k] + tm * cols_dev
-        for i in range(0, cols_dev, 64):
+
+        def piece(i):
             base = pattern_o + ((col0 + i) * C_A + seeds[0] * C_S)
             omega[k * cols_dev + i : k * cols_dev + i + 64, :] = gauss(base, col_factor)
 
+        return [functools.partial(piece, i) for i in range(0, cols_dev, 64)]
+
     def xi_hash(k):
         col0 = offsets[k] + tm * cols_dev
-        for i in range(0, cols_dev, 64):
-            for g in range(0, CORE, 128):
-                base = pattern_x + ((col0 + i) * C_B + seeds[3] * C_S + wrapped(g * C_A))
-                xit[k * cols_dev + i : k * cols_dev + i + 64, g : g + 128] = gauss(base, col_factor)
+
+        def piece(i, g):
+            base = pattern_x + ((col0 + i) * C_B + seeds[3] * C_S + wrapped(g * C_A))
+            xit[k * cols_dev + i : k * cols_dev + i + 64, g : g + 128] = gauss(base, col_factor)
+
+        return [functools.partial(piece, i, g) for i in range(0, cols_dev, 64) for g in range(0, CORE, 128)]
 
     def make_ids():
         m = iota((CORE, 128), 0)
@@ -150,51 +170,62 @@
         psi_ids[...] = row * C_A + iota((CORANGE, 128), 1) * C_B
 
     def row_hash(kc, ids, lhs, seed):
-        for g in range(0, KC, 128):
+        def piece(g, r):
             shift = (row0 + (kc * KC + g)) * C_B + seed * C_S
-            for r in range(0, ids.shape[0], 64):
-                lhs[r : r + 64, g : g + 128] = gauss(ids[r : r + 64, :] + shift, row_factor)
+            lhs[r : r + 64, g : g + 128] = gauss(ids[r : r + 64, :] + shift, row_factor)
+
+        return [functools.partial(piece, g, r) for g in range(0, KC, 128) for r in range(0, ids.shape[0], 64)]
 
     def phi_hash(kc):
-        row_hash(kc, phi_ids, (phi_lhs0, phi_lhs1)[kc % 2], seeds[2])
+        return row_hash(kc, phi_ids, (phi_lhs0, phi_lhs1)[kc % 2], seeds[2])
 
     def psi_hash(kc):
-        row_hash(kc, psi_ids, psi_lhs.at[:, kc * KC : (kc + 1) * KC], seeds[1])
+        return row_hash(kc, psi_ids, psi_lhs.at[:, kc * KC : (kc + 1) * KC], seeds[1])
 
     def phi_dot(kc):
-        for k in range(blocks):
-            for n in range(0, cols_dev, 256):
-                got = jnp.dot(
-                    (phi_lhs0, phi_lhs1)[kc % 2][...],
-                    rec[k, kc * KC : (kc + 1) * KC, n : n + 256],
-                    preferred_element_type=jnp.float32,
-                )
-                at = slice(k * cols_dev + n, k * cols_dev + n + 256)
-                proj[:, at] = got if kc == 0 else proj[:, at] + got
+        def piece(k, n):
+            got = jnp.dot(
+                (phi_lhs0, phi_lhs1)[kc % 2][...],
+                rec[k, kc * KC : (kc + 1) * KC, n : n + 256],
+                preferred_element_type=jnp.float32,
+            )
+            at = slice(k * cols_dev + n, k * cols_dev + n + 256)
+            proj[:, at] = got if kc == 0 else proj[:, at] + got
+
+        return [functools.partial(piece, k, n) for k in range(blocks) for n in range(0, cols_dev, 256)]
 
     def psi_dot(k):
-        for n in range(0, cols_dev, 256):
+        def piece(n):
             cor[:, k * cols_dev + n : k * cols_dev + n + 256] = jnp.dot(
                 psi_lhs[...], rec[k, :, n : n + 256], preferred_element_type=jnp.float32
             )
 
-    def core_dot(r0, rows):
-        part_of = proj[r0 : r0 + rows, :]
-        high = part_of.astype(jnp.bfloat16)
-        low = (part_of - high.astype(jnp.float32)).astype(jnp.bfloat16)
-        core[r0 : r0 + rows, :] = jnp.dot(
-            high, xit[...], preferred_element_type=jnp.float32
-        ) + jnp.dot(low, xit[...], preferred_element_type=jnp.float32)
-
-    def range_chunk(d):
-        where = pl.ds(pl.multiple_of(d * chunk, chunk), chunk)
-        part[where, :] = jnp.dot(
-            rec[0, where, :], omega[0:cols_dev, :], preferred_element_type=jnp.float32
-        ) + jnp.dot(
-            rec[1, where, :], omega[cols_dev : 2 * cols_dev, :], preferred_element_type=jnp.float32
-        )
-
-    Z, D = {}, {}
+        return [functools.partial(piece, n) for n in range(0, cols_dev, 256)]
+
+    def core_dot(r0):
+        def piece():
+            part_of = proj[r0 : r0 + HALF_PHI, :]
+            high = part_of.astype(jnp.bfloat16)
+            low = (part_of - high.astype(jnp.float32)).astype(jnp.bfloat16)
+            got = jnp.dot(
+                jnp.concatenate([high, low], axis=0), xit[...], preferred_element_type=jnp.float32
+            )
+            core[r0 : r0 + HALF_PHI, :] = got[0:HALF_PHI] + got[HALF_PHI : 2 * HALF_PHI]
+
+        return [piece]
+
+    def range_dot(d):
+        def piece(i):
+            where = pl.ds(pl.multiple_of(d * chunk + i, 256), 256)
+            part[where, :] = jnp.dot(
+                rec[0, where, :], omega[0:cols_dev, :], preferred_element_type=jnp.float32
+            ) + jnp.dot(
+                rec[1, where, :], omega[cols_dev : 2 * cols_dev, :], preferred_element_type=jnp.float32
+            )
+
+        return [functools.partial(piece, i) for i in range(0, chunk, 256)]
+
+    D = {}
 
     def range_forward(s):
         arrive(rb1.at[s], s1r.at[s])
@@ -234,33 +265,63 @@
     def range_end():
         arrive(range_out.at[0 : (2 * (STREAMS - 1) + 6) * run], g2r.at[0])
 
-    def z_step(what, step, up):
-        d = lax.rem(z + (5 - step) if up else z + ZS - 5 + step, ZS)
+    def cor_of(d, b, row, rows):
+        cols = slice(b * cols_dev, (b + 1) * cols_dev)
+        at = pl.ds(pl.multiple_of(d * 16 + row, 8), rows)
+        mine = pl.ds(pl.multiple_of(HALF_PSI + d * 16 + row, 8), rows)
+        return cor[mine, cols] + got_cor[at, cols]
+
+    def cor_step(b, up, step):
         way = 0 if up else 1
-        at = pl.ds(pl.multiple_of(d * (24 if what else 16), 8), 24 if what else 16)
-        i = step - 1
+        total = cor_of(lax.rem(z + (5 - step) if up else z + ZS - 5 + step, ZS), b, 0, 16)
+        if step > (1 if b == way else 2):
+            arrive(zr_cor.at[b, way, step - 2], zr.at[b, way, step - 2])
+            total = total + zr_cor[b, way, step - 2]
+        zs_cor[b, way, step - 1] = total
+        if step < 4:
+            send(
+                1, zs_cor.at[b, way, step - 1], zr_cor.at[b, way, step - 1], zr.at[b, way, step - 1],
+                z_up if up else z_down,
+            )
+        else:
+            for other, to in ((0, z_up if up else z_down), (1, z_up_x if up else z_down_x)):
+                row = xl * 8 if other == 0 else (1 - xl) * 8
+                rows = pl.ds(pl.multiple_of(row, 8), 8)
+                send(1, zs_cor.at[b, way, 3, rows], fin.at[b, 2 * way + other], fr.at[b], to)
+
+    def cor_other(b):
+        zs_own[b] = cor_of(z, b, (1 - xl) * 8, 8)
+        send(1, zs_own.at[b], fin.at[b, 4], fr.at[b], xl_peer)
+
+    def cor_final(b):
+        arrive(fin.at[b], fr.at[b])
+        corange_out[b] = (
+            cor_of(z, b, xl * 8, 8) + fin[b, 4] + (fin[b, 0] + fin[b, 1]) + (fin[b, 2] + fin[b, 3])
+        )
+
+    def core_own(d):
+        at = pl.ds(pl.multiple_of(d * 24, 8), 24)
+        mine = pl.ds(pl.multiple_of(HALF_PHI + d * 24, 8), 24)
+        return core[mine, :] + got_core[at, :]
+
+    def core_gather(up):
+        way = 0 if up else 1
+        rows = slice(0, 16) if up else slice(16, 24)
         to = z_up if up else z_down
-        if what:
-            kept, got, sums, arrived = core.at[HALF_PHI:CORE], got_core, zs_core, zr_core
-            pick = (slice(0, 16) if up else slice(16, 24), slice(None))
-        else:
-            kept, got, sums, arrived = cor.at[HALF_PSI:CORANGE], got_cor, zs_cor, zr_cor
-            pick = (slice(None), slice(0, cols_dev) if up else slice(cols_dev, 2 * cols_dev))
-        if step == 1:
-            rows, cols = pick
-            at = pl.ds(pl.multiple_of(d * 24 + rows.start, 8), rows.stop - rows.start) if what else at
-            sums[(way, 0, *pick)] = kept[at, cols] + got[at, cols]
-        else:
-            Z[what, step - 1, way].wait_recv()
-            total = kept[at, :] + got[at, :]
-            if step > 2:
-                total = total + arrived[way, i - 1]
-            sums[way, i] = total
-            if step == 2:
-                sums[(way, i, *pick)] += arrived[(way, 0, *pick)]
-        pick = (way, i, *pick) if step == 1 else (way, i)
-        sem = zr.at[what, 6 if step == 4 else 3 * way + i]
-        Z[what, step, way] = send(1, sums.at[pick], arrived.at[pick], sem, to)
+        zs_core[way, 0] = core_own(lax.rem(z + 4, ZS))
+        zs_core[way, 1] = core_own(lax.rem(z + (2 if up else ZS - 2), ZS))
+        send(1, zs_core.at[way, 0, rows], zr_core.at[way, 0, rows], kr.at[way], to)
+        send(1, zs_core.at[way, 1], zr_core.at[way, 1], kr.at[way], to)
+
+    def core_deliver(up):
+        way = 0 if up else 1
+        rows = slice(0, 16) if up else slice(16, 24)
+        arrive(core.at[0 : 40 if up else 32], kr.at[way])
+        zs_core[way, 2] = core_own(lax.rem(z + (3 if up else ZS - 3), ZS))
+        zs_core[way, 2, rows, :] += zr_core[way, 0, rows, :]
+        zs_core[way, 3] = core_own(lax.rem(z + (1 if up else ZS - 1), ZS)) + zr_core[way, 1]
+        send(1, zs_core.at[way, 2], zr_core.at[way, 2], kr.at[2], z_up3 if up else z_down3)
+        send(1, zs_core.at[way, 3], zr_core.at[way, 3], kr.at[2], z_up if up else z_down)
 
     def pair(what, src, dst):
         D[what] = send(2, src, dst, dr.at[what], partner)
@@ -268,12 +329,10 @@
     make_ids()
     for load in scalars:
         load.wait()
-    omega_hash(0)
-    omega_hash(1)
-    xi_hash(0)
+    xi = xi_hash(0) + xi_hash(1)
+    run_all(omega_hash(0) + omega_hash(1) + xi[0:2])
     loads[0].wait()
-    range_chunk(y_far)
-    xi_hash(1)
+    together(range_dot(y_far), xi[2:16])
     pl.semaphore_wait(barrier, len(greeted))
     send(0, part.at[rows_of(y_far, 0)], rb0.at[0], cr.at[0], far)
     for s in range(1, STREAMS):
@@ -281,70 +340,46 @@
         send(0, part.at[rows_of(y_far, s, 1)], rb1.at[s, 1], s1r.at[s], left)
     for load in loads[1:]:
         load.wait()
-    phi_hash(0)
-    range_chunk(y_right)
-    range_chunk(y_left)
+    together(range_dot(y_right) + range_dot(y_left), xi[16:] + phi_hash(0))
     send(0, part.at[rows_of(y_right, 0)], rb0.at[1], cr.at[0], right)
     send(0, part.at[rows_of(y_left, 0)], rb0.at[2], cr.at[0], left)
     for s in range(1, STREAMS):
         send(0, part.at[rows_of(y_right, s, 1)], rb2.at[s, 0], cr.at[s], right)
         send(0, part.at[rows_of(y_left, s, 0)], rb2.at[s, 1], cr.at[s], left)
-    phi_hash(1)
-    phi_dot(0)
-    phi_hash(2)
-    phi_dot(1)
-    phi_hash(3)
-    phi_dot(2)
-    psi_hash(0)
-    phi_dot(3)
-    core_dot(0, HALF_PHI)
+    run_all(phi_hash(1) + phi_dot(0) + phi_hash(2) + phi_dot(1) + phi_hash(3) + phi_dot(2) + psi_hash(0)[0:8] + phi_dot(3) + psi_hash(0)[8:] + core_dot(0))
     pair(2, core.at[0:HALF_PHI], got_core)
+    run_all(psi_hash(1) + core_dot(HALF_PHI))
     range_forward(1)
-    range_chunk(y)
-    psi_hash(1)
-    core_dot(HALF_PHI, HALF_PHI)
-    psi_hash(2)
+    run_all(psi_hash(2) + range_dot(y) + psi_hash(3))
+    D[2].wait_recv()
+    core_gather(True)
+    core_gather(False)
     range_forward(2)
     range_forward(3)
-    psi_hash(3)
+    run_all(psi_dot(0))
+    pair(0, cor.at[0:HALF_PSI, 0:cols_dev], got_cor.at[:, 0:cols_dev])
+    run_all(psi_dot(1))
+    pair(1, cor.at[0:HALF_PSI, cols_dev : 2 * cols_dev], got_cor.at[:, cols_dev : 2 * cols_dev])
     range_cross(0)
-    D[2].wait_recv()
-    z_step(1, 1, True)
-    z_step(1, 1, False)
-    psi_dot(0)
-    pair(0, cor.at[0:HALF_PSI, 0:cols_dev], got_cor.at[:, 0:cols_dev])
-    psi_dot(1)
-    pair(1, cor.at[0:HALF_PSI, cols_dev : 2 * cols_dev], got_cor.at[:, cols_dev : 2 * cols_dev])
     D[0].wait_recv()
-    z_step(0, 1, True)
+    cor_step(0, True, 1)
+    cor_step(0, False, 2)
+    cor_other(0)
+    range_cross(1)
     D[1].wait_recv()
-    z_step(0, 1, False)
-    z_step(1, 2, True)
-    z_step(1, 2, False)
-    range_cross(1)
+    cor_step(1, True, 2)
+    cor_step(1, False, 1)
+    cor_other(1)
     range_cross(2)
+    core_deliver(True)
+    core_deliver(False)
+    range_cross(3)
     range_spread(0)
-    range_cross(3)
-    z_step(0, 2, True)
-    z_step(0, 2, False)
-    z_step(1, 3, True)
-    z_step(1, 3, False)
-    own_cor = pl.ds(pl.multiple_of(HALF_PSI + z * 16, 16), 16)
-    own_core = pl.ds(pl.multiple_of(HALF_PHI + z * 24, 8), 24)
-    core[own_core, :] += got_core[pl.ds(pl.multiple_of(z * 24, 8), 24), :]
-    cor[own_cor, :] += got_cor[pl.ds(pl.multiple_of(z * 16, 16), 16), :]
+    for b, up, step in ((0, True, 2), (0, False, 3), (1, False, 2), (1, True, 3)):
+        cor_step(b, up, step)
     range_spread(1)
-    z_step(0, 3, True)
-    z_step(0, 3, False)
-    range_relay(0)
-    range_spread(2)
-    z_step(1, 4, True)
-    z_step(1, 4, False)
-    range_spread(3)
-    z_step(0, 4, True)
-    z_step(0, 4, False)
-    arrive(zr_core.at[0:2, 3], zr.at[1, 6])
-    both = core[own_core, :] + zr_core[0, 3] + zr_core[1, 3]
+    arrive(zr_core.at[0:2, 2:4], kr.at[2])
+    both = core_own(z) + (zr_core[0, 2] + zr_core[0, 3]) + (zr_core[1, 2] + zr_core[1, 3])
     pad = jnp.zeros((4, CORE), jnp.float32)
     for i in range(2):
         shares[i, 0:12, :] = both[i * 12 : i * 12 + 12, :]
@@ -354,23 +389,24 @@
     send(2, shares.at[xl], xg.at[me_x], tr.at[0], x_peer)
     send(2, shares.at[1 - xl], xg.at[me_x], tr.at[0], xx_peer)
     xg[me_x] = shares[xl]
-    range_relay(1)
+    range_spread(2)
+    for b, up, step in ((0, True, 3), (0, False, 4), (1, False, 3), (1, True, 4)):
+        cor_step(b, up, step)
+    range_relay(0)
+    range_spread(3)
     arrive(xg.at[0:3], tr.at[0])
     yg[y] = (xg[0] + xg[1]) + (xg[2] + xg[3])
     for to in (right, left, far):
         send(2, yg.at[y], yg.at[y], ur.at[0], to)
-    arrive(zr_cor.at[0:2, 3], zr.at[0, 6])
-    cor[own_cor, :] += zr_cor[0, 3] + zr_cor[1, 3]
-    other = pl.ds(pl.multiple_of(HALF_PSI + z * 16 + (1 - xl) * 8, 8), 8)
-    send(2, cor.at[other], xl_cor, lr.at[0], xl_peer)
+    range_relay(1)
+    cor_step(0, True, 4)
+    cor_step(1, False, 4)
     range_relay(2)
-    arrive(xl_cor, lr.at[0])
-    mine = cor[pl.ds(pl.multiple_of(HALF_PSI + z * 16 + xl * 8, 8), 8), :] + xl_cor[...]
-    for k in range(blocks):
-        corange_out[k] = mine[:, k * cols_dev : (k + 1) * cols_dev]
     arrive(yg.at[0:3], ur.at[0])
     total = (yg[0] + yg[1]) + (yg[2] + yg[3])
     core_out[...] = total[0:12, :]
+    cor_final(0)
+    cor_final(1)
     range_end()
     for group, ref in enumerate((rec, part, rec)):
         rows = sent[group] // (ref.shape[-1] * ref.dtype.itemsize)
@@ -431,11 +467,12 @@
             vmem((STREAMS, 2 * run, RANGE), f32),
             vmem((HALF_PSI, blocks * cols_dev), f32),
             vmem((HALF_PHI, CORE), f32),
-            vmem((2, 4, 16, blocks * cols_dev), f32),
+            vmem((blocks, 2, 3, 16, cols_dev), f32),
             vmem((2, 4, 24, CORE), f32),
-            vmem((2, 4, 16, blocks * cols_dev), f32),
+            vmem((blocks, 2, 4, 16, cols_dev), f32),
             vmem((2, 4, 24, CORE), f32),
-            vmem((8, blocks * cols_dev), f32),
+            vmem((blocks, 8, cols_dev), f32),
+            vmem((blocks, 5, 8, cols_dev), f32),
             vmem((2, 16, CORE), f32),
             vmem((4, 16, CORE), f32),
             vmem((YS, 16, CORE), f32),
@@ -447,8 +484,9 @@
             dma((STREAMS - 1,)),
             dma((1,)),
             dma((3,)),
-            dma((2, 7)),
-            dma((1,)),
+            dma((blocks, 2, 3)),
+            dma((blocks,)),
+            dma((3,)),
             dma((1,)),
             dma((1,)),
         ],

time: 40 us -> 37 us (0.925); the launches traced: 39.7 us -> 36.3 us
  Pallas kernels: 39.1 us -> 35.7 us
    pallas_call x1, Pallas kernels: 38.1 us -> 34.7 us  [shards(): pl.pallas_call(functools.partial(kernel, row_factor, col_factor, rows_dev...]
where the time goes in v4:
time: 37 us; the launch traced here: 36.3 us
  Pallas kernels  35.7 us (96%)
  between operations  0.64 us (2%)
    pallas_call x1, Pallas kernels, shards(): pl.pallas_call(functools.partial(kernel, row_factor, col_factor, rows_dev...  34.7 us
    pallas_call x1, Pallas kernels, shards(): pl.pallas_call(put_out, out_shape=tuple((jax.ShapeDtypeStruct(shape, f32)...  1 us

profile of v4, /device:TPU:32, one launch (start us, length us, event | category | flops | bytes accessed | tf_op | source)
XLA Modules:
  0.0 36.3 jit_solution(4201531317046363047)
XLA Ops:
  0.6 34.7 %three_sketch.1 = (f32[2048,128]{1,0:T(8,128)S(1)}, f32[2,8,512]{2,1,0:T(8,128)S(1)}, f32[12,384]{1,0:T(8,128)S(1)}) custom-call(s32[4]{0:T(128)} %seeds_in.1, s32[2]{0:T(128)} %offsets_in.1, bf16[2,2048,512]{2,1,0:T(8,128)(2,1)} %record.1), custom_call_target="tpu_custom_call" | custom-call | tf_op jit(solution)/shard_map/three_sketch/pallas_call | solution.py:438
  35.3 1.0 %put_out.1 = (f32[2048,128]{1,0:T(8,128)}, f32[2,8,512]{2,1,0:T(8,128)}, f32[12,384]{1,0:T(8,128)}) custom-call(f32[2048,128]{1,0:T(8,128)S(1)} %get-tuple-element.6.refs_0_, f32[2,8,512]{2,1,0:T(8,128)S(1)} %get-tuple-element.7.refs_1_, f32[12,384]{1,0:T(8,128)S(1)} %get-tuple-element.8.refs_2_), custom_call_target="tpu_custom_call" | custom-call | tf_op jit(solution)/shard_map/put_out/pallas_call | solution.py:496

commit v5 on v4

--- a/solution.py
+++ b/solution.py
@@ -75,6 +75,10 @@
     far = device(y=y_far)
     xx_peer = device(xh=1 - xh, xl=1 - xl)
 
+    barrier = pltpu.get_barrier_semaphore()
+    greeted = [z_up3, z_down3, far, x_peer, z_up_x, z_down_x, z_up, z_down, xl_peer, xx_peer, right, left, partner]
+    for other in greeted:
+        pl.semaphore_signal(barrier, inc=1, device_id=other, device_id_type=MESH)
     scalars = [
         pltpu.make_async_copy(seeds_in, seeds, in_sem.at[YS]),
         pltpu.make_async_copy(offsets_in, offsets, in_sem.at[YS + 1]),
@@ -90,10 +94,6 @@
         load.start()
         loads.append(load)
 
-    barrier = pltpu.get_barrier_semaphore()
-    greeted = [partner, z_up, z_down, z_up3, z_down3, z_up_x, z_down_x, xl_peer, x_peer, xx_peer, right, left, far]
-    for other in greeted:
-        pl.semaphore_signal(barrier, inc=1, device_id=other, device_id_type=MESH)
 
     run = chunk // STREAMS // 2
 
@@ -333,6 +333,7 @@
     run_all(omega_hash(0) + omega_hash(1) + xi[0:2])
     loads[0].wait()
     together(range_dot(y_far), xi[2:16])
+    run_all(xi[16:32])
     pl.semaphore_wait(barrier, len(greeted))
     send(0, part.at[rows_of(y_far, 0)], rb0.at[0], cr.at[0], far)
     for s in range(1, STREAMS):
@@ -340,7 +341,7 @@
         send(0, part.at[rows_of(y_far, s, 1)], rb1.at[s, 1], s1r.at[s], left)
     for load in loads[1:]:
         load.wait()
-    together(range_dot(y_right) + range_dot(y_left), xi[16:] + phi_hash(0))
+    together(range_dot(y_right) + range_dot(y_left), xi[32:] + phi_hash(0))
     send(0, part.at[rows_of(y_right, 0)], rb0.at[1], cr.at[0], right)
     send(0, part.at[rows_of(y_left, 0)], rb0.at[2], cr.at[0], left)
     for s in range(1, STREAMS):
@@ -350,10 +351,11 @@
     pair(2, core.at[0:HALF_PHI], got_core)
     run_all(psi_hash(1) + core_dot(HALF_PHI))
     range_forward(1)
-    run_all(psi_hash(2) + range_dot(y) + psi_hash(3))
+    run_all(psi_hash(2) + range_dot(y))
     D[2].wait_recv()
     core_gather(True)
     core_gather(False)
+    run_all(psi_hash(3))
     range_forward(2)
     range_forward(3)
     run_all(psi_dot(0))
@@ -385,8 +387,8 @@
         shares[i, 0:12, :] = both[i * 12 : i * 12 + 12, :]
         shares[i, 12:16, :] = pad
     me_x = xh * 2 + xl
+    send(2, shares.at[xl], xg.at[me_x], tr.at[0], x_peer)
     send(2, shares.at[1 - xl], xg.at[me_x], tr.at[0], xl_peer)
-    send(2, shares.at[xl], xg.at[me_x], tr.at[0], x_peer)
     send(2, shares.at[1 - xl], xg.at[me_x], tr.at[0], xx_peer)
     xg[me_x] = shares[xl]
     range_spread(2)
@@ -396,7 +398,7 @@
     range_spread(3)
     arrive(xg.at[0:3], tr.at[0])
     yg[y] = (xg[0] + xg[1]) + (xg[2] + xg[3])
-    for to in (right, left, far):
+    for to in (far, right, left):
         send(2, yg.at[y], yg.at[y], ur.at[0], to)
     range_relay(1)
     cor_step(0, True, 4)

time: 37 us -> 37 us (level)
  the two profiles are of different devices: /device:TPU:32 before, /device:TPU:1 now
where the time goes in v5:
time: 37 us
  Pallas kernels  36.3 us (98%)
  between operations  0.64 us (2%)
    pallas_call x1, Pallas kernels, shards(): pl.pallas_call(functools.partial(kernel, row_factor, col_factor, rows_dev...  35.3 us
    pallas_call x1, Pallas kernels, shards(): pl.pallas_call(put_out, out_shape=tuple((jax.ShapeDtypeStruct(shape, f32)...  1 us

profile of v5, /device:TPU:1, one launch (start us, length us, event | category | flops | bytes accessed | tf_op | source)
XLA Modules:
  0.0 37.0 jit_solution(16703622900896102575)
XLA Ops:
  0.6 35.3 %three_sketch.1 = (f32[2048,128]{1,0:T(8,128)S(1)}, f32[2,8,512]{2,1,0:T(8,128)S(1)}, f32[12,384]{1,0:T(8,128)S(1)}) custom-call(s32[4]{0:T(128)} %seeds_in.1, s32[2]{0:T(128)} %offsets_in.1, bf16[2,2048,512]{2,1,0:T(8,128)(2,1)} %record.1), custom_call_target="tpu_custom_call" | custom-call | tf_op jit(solution)/shard_map/three_sketch/pallas_call | solution.py:440
  36.0 1.0 %put_out.1 = (f32[2048,128]{1,0:T(8,128)}, f32[2,8,512]{2,1,0:T(8,128)}, f32[12,384]{1,0:T(8,128)}) custom-call(f32[2048,128]{1,0:T(8,128)S(1)} %get-tuple-element.6.refs_0_, f32[2,8,512]{2,1,0:T(8,128)S(1)} %get-tuple-element.7.refs_1_, f32[12,384]{1,0:T(8,128)S(1)} %get-tuple-element.8.refs_2_), custom_call_target="tpu_custom_call" | custom-call | tf_op jit(solution)/shard_map/put_out/pallas_call | solution.py:498

commit v6 on v5

--- a/solution.py
+++ b/solution.py
@@ -367,14 +367,14 @@
     cor_step(0, True, 1)
     cor_step(0, False, 2)
     cor_other(0)
-    range_cross(1)
     D[1].wait_recv()
     cor_step(1, True, 2)
     cor_step(1, False, 1)
     cor_other(1)
-    range_cross(2)
     core_deliver(True)
     core_deliver(False)
+    range_cross(1)
+    range_cross(2)
     range_cross(3)
     range_spread(0)
     for b, up, step in ((0, True, 2), (0, False, 3), (1, False, 2), (1, True, 3)):

time: 37 us -> 37.8 us (1.022)
  Pallas kernels: 36.3 us -> 37.1 us
    pallas_call x1, Pallas kernels: 35.3 us -> 36.1 us  [shards(): pl.pallas_call(functools.partial(kernel, row_factor, col_factor, rows_dev...]
where the time goes in v6:
time: 37.8 us; the launch traced here: 37.7 us
  Pallas kernels  37.1 us (98%)
  between operations  0.64 us (2%)
    pallas_call x1, Pallas kernels, shards(): pl.pallas_call(functools.partial(kernel, row_factor, col_factor, rows_dev...  36.1 us
    pallas_call x1, Pallas kernels, shards(): pl.pallas_call(put_out, out_shape=tuple((jax.ShapeDtypeStruct(shape, f32)...  1 us

profile of v6, /device:TPU:1, one launch (start us, length us, event | category | flops | bytes accessed | tf_op | source)
XLA Modules:
  0.0 37.7 jit_solution(8321348211458982558)
XLA Ops:
  0.6 36.1 %three_sketch.1 = (f32[2048,128]{1,0:T(8,128)S(1)}, f32[2,8,512]{2,1,0:T(8,128)S(1)}, f32[12,384]{1,0:T(8,128)S(1)}) custom-call(s32[4]{0:T(128)} %seeds_in.1, s32[2]{0:T(128)} %offsets_in.1, bf16[2,2048,512]{2,1,0:T(8,128)(2,1)} %record.1), custom_call_target="tpu_custom_call" | custom-call | tf_op jit(solution)/shard_map/three_sketch/pallas_call | solution.py:440
  36.7 1.0 %put_out.1 = (f32[2048,128]{1,0:T(8,128)}, f32[2,8,512]{2,1,0:T(8,128)}, f32[12,384]{1,0:T(8,128)}) custom-call(f32[2048,128]{1,0:T(8,128)S(1)} %get-tuple-element.6.refs_0_, f32[2,8,512]{2,1,0:T(8,128)S(1)} %get-tuple-element.7.refs_1_, f32[12,384]{1,0:T(8,128)S(1)} %get-tuple-element.8.refs_2_), custom_call_target="tpu_custom_call" | custom-call | tf_op jit(solution)/shard_map/put_out/pallas_call | solution.py:498
